TPU v7x, 256 devices: a whole 4x4x8 slice. The times are simulated.
256 devices in a mesh: gz: 32 (over x, y, core), xy: 8 (over z).
Axes of the slice: x: 4, y: 4, z: 8, core: 2. Of those that a mesh axis runs over, the one named last changes fastest.
Arguments:
- east_velocity: float32 [512, 256, 512], P('xy', 'gz'), may hold values from -6 to 6
- north_velocity: float32 [512, 256, 512], P('xy', 'gz'), may hold values from -6 to 6
- upward_velocity: float32 [512, 256, 512], P('xy', 'gz'), may hold values from -5 to 5
- obstacle: int32 [512, 256, 512], P('xy', 'gz'), may hold values 0 or 1
Outputs:
- east_corrected: float32 [512, 256, 512], P('xy', 'gz')
- north_corrected: float32 [512, 256, 512], P('xy', 'gz')
- upward_corrected: float32 [512, 256, 512], P('xy', 'gz')
- pressure: float32 [512, 256, 512], P('xy', 'gz')
- residual: float32 [512, 256, 512], P('xy', 'gz')
All inputs are finite; a program needn't handle non-finite values. No bound on the sum of `obstacle` on one device may be relied on, other than what follows from the above.
Results may differ from a plain program's by a relative error of at most 0.0003.
Values sent between devices are 32-bit elements; how exact they have to be, the bound alone decides.
A program may use at most 128 MiB of HBM per device.

v0:
```python
import jax
import jax.numpy as jnp
from jax import lax
from jax.sharding import Mesh
from jax.sharding import PartitionSpec as P

NX = 512
NY = 512
CZ = 8
GZ = ("gz_0", "gz_1", "gz_2")


HIGH = lax.Precision.HIGHEST


def extended(shard, sides, width):
    edges = {}
    for axis, dim in sides:
        peers, length = (lax.axis_size(axis), shard.shape[dim])
        up = [(i, (i + 1) % peers) for i in range(peers)]
        last = lax.slice_in_dim(shard, length - width, length, axis=dim)
        initial = lax.slice_in_dim(shard, 0, width, axis=dim)
        edges[dim] = (
            lax.ppermute(last, axis, up),
            lax.ppermute(initial, axis, [(b, a) for a, b in up]),
        )
    done = []
    for _, dim in sides:
        low, high = edges[dim]
        around = [(width, width) if d in done else (0, 0) for d in range(shard.ndim)]
        shard = jnp.concatenate([jnp.pad(low, around), shard, jnp.pad(high, around)], axis=dim)
        done.append(dim)
    return shard


def split_up(shard, dim, peers):
    before, after = (shard.shape[:dim], shard.shape[dim + 1 :])
    return jnp.moveaxis(shard.reshape(*before, peers, -1, *after), dim, 0)


def in_order(tiles, dim):
    tiles = jnp.moveaxis(tiles, 0, dim)
    dims = tiles.shape
    return tiles.reshape(*dims[:dim], dims[dim] * dims[dim + 1], *dims[dim + 2 :])


def turned_blocks(tiles, axes, order):
    dims = [lax.axis_size(a) for a in axes]
    tiles = tiles.reshape(*dims, *tiles.shape[1:])
    for k in order:
        tiles = lax.all_to_all(tiles, axes[k], split_axis=k, concat_axis=k, tiled=True)
    return tiles.reshape(-1, *tiles.shape[len(axes) :])


def two_step_exchange(shard, groups, order, split_dim, concat_dim):
    peers = lax.axis_size(groups[0]) * lax.axis_size(groups[1])
    tiles = split_up(shard, split_dim, peers)
    return in_order(turned_blocks(tiles, groups, order), concat_dim)


def hartley(length):
    index = jnp.arange(length, dtype=jnp.int32)
    product = index[:, None] * index[None, :] % length
    angle = 2.0 * jnp.pi / length * product.astype(jnp.float32)
    return jnp.cos(angle) + jnp.sin(angle)


def eigenvalues(length):
    index = jnp.arange(length, dtype=jnp.int32).astype(jnp.float32)
    return 2.0 - 2.0 * jnp.cos(2.0 * jnp.pi / length * index)


def tridiagonal(diagonal, right):
    start = jnp.zeros_like(right[0])

    def tridiagonal_forward(carry, plane):
        ratio, value = carry
        divisor = diagonal + ratio
        ratio_new = -1.0 / divisor
        value_new = (plane + value) / divisor
        return ((ratio_new, value_new), (ratio_new, value_new))

    _, (ratios, values) = lax.scan(tridiagonal_forward, (start, start), right)

    def tridiagonal_backward(after, pair):
        ratio, value = pair
        solution = value - ratio * after
        return (solution, solution)

    _, solved = lax.scan(tridiagonal_backward, start, (ratios, values), reverse=True)
    return solved


def interface_chain(bottoms, tops, couple, spread):
    start = jnp.zeros_like(bottoms[0] * couple)

    def interface_forward(carry, pair):
        slope, offset = carry
        bottom, top = pair
        divisor = 1.0 - couple * slope
        slope_new = couple + spread * spread * slope / divisor
        offset_new = top + spread * offset + spread * slope * (bottom + couple * offset) / divisor
        return ((slope_new, offset_new), (slope, offset))

    _, (slopes, offsets) = lax.scan(interface_forward, (start, start), (bottoms, tops))

    def interface_backward(above, items):
        slope, offset, bottom, top = items
        lower = (bottom + couple * offset + spread * above) / (1.0 - couple * slope)
        upper = top + spread * (slope * lower + offset) + couple * above
        return (lower, (lower, upper))

    _, (lowers, uppers) = lax.scan(
        interface_backward, start, (slopes, offsets, bottoms, tops), reverse=True
    )
    return (lowers, uppers)


def local(east_velocity, north_velocity, upward_velocity, obstacle):
    groups = lax.axis_size("xy")
    slabs = lax.axis_size(GZ)
    east_rows = NX // groups
    north_rows = NY // groups
    group_index = lax.axis_index("xy")
    slab_index = lax.axis_index(GZ)
    first_slab = slab_index == 0
    last_slab = slab_index == slabs - 1
    fluid = (1 - obstacle).astype(jnp.float32)
    stacked = jnp.stack([east_velocity, upward_velocity, fluid])
    framed = extended(stacked, ((GZ, 2), ("xy", 1)), 1)
    inner = framed[:, :, 1:-1]
    east_next = inner[0, -1]
    fluid_west = inner[2, 0]
    fluid_east = inner[2, -1]
    column = framed[:, 1:-1]
    upward_above = jnp.where(last_slab, 0.0, column[1, :, -1])
    fluid_below = jnp.where(first_slab, 1.0, column[2, :, 0])
    fluid_above = jnp.where(last_slab, 0.0, column[2, :, -1])
    open_east = fluid * jnp.concatenate([fluid_west[None], fluid[:-1]], 0)
    open_north = fluid * jnp.roll(fluid, 1, 2)
    open_up = fluid * jnp.concatenate([fluid_below[:, None], fluid[:, :-1]], 1)
    east_masked = open_east * east_velocity
    north_masked = open_north * north_velocity
    upward_masked = open_up * upward_velocity
    east_after = jnp.concatenate([east_masked[1:], (east_next * fluid_east * fluid[-1])[None]], 0)
    upward_after = jnp.concatenate(
        [upward_masked[:, 1:], (upward_above * fluid_above * fluid[:, -1])[:, None]], 1
    )
    source = (
        east_masked
        - east_after
        + (north_masked - jnp.roll(north_masked, -1, 2))
        + (upward_masked - upward_after)
    )
    table_east = hartley(NX).reshape(groups, east_rows, NX)
    table_north = hartley(NY).reshape(groups, north_rows, NY)
    sorted_modes = jnp.einsum("xzy,gky->gxzk", source, table_north, precision=HIGH).reshape(
        groups, east_rows, CZ * north_rows
    )
    received = lax.all_to_all(sorted_modes, "xy", split_axis=0, concat_axis=0, tiled=True)
    spectrum = jnp.einsum("gxm,gxa->ma", received, table_east, precision=HIGH).reshape(
        CZ, north_rows, NX
    )
    north_modes = group_index * north_rows + jnp.arange(north_rows, dtype=jnp.int32)
    north_eigen = 2.0 - 2.0 * jnp.cos(2.0 * jnp.pi / NY * north_modes.astype(jnp.float32))
    diagonal = 2.0 + north_eigen[:, None] + eigenvalues(NX)[None, :]
    unit = jnp.broadcast_to(
        (jnp.arange(CZ) == 0).astype(jnp.float32)[:, None, None], spectrum.shape
    )
    solved = tridiagonal(diagonal, jnp.stack([spectrum, unit], 1))
    local_part = solved[:, 0]
    spike = solved[:, 1]
    couple = spike[0]
    spread = spike[-1]
    ends = jnp.stack([local_part[0], local_part[-1]])
    modes = north_rows * NX
    share = modes // slabs
    flat_ends = ends.reshape(1, 2, modes)
    arrived = two_step_exchange(flat_ends, (("gz_0", "gz_1"), "gz_2"), (1, 0), 2, 0)
    couple_share = lax.dynamic_slice_in_dim(couple.reshape(modes), slab_index * share, share)
    spread_share = lax.dynamic_slice_in_dim(spread.reshape(modes), slab_index * share, share)
    lowers, uppers = interface_chain(arrived[:, 0], arrived[:, 1], couple_share, spread_share)
    blank_row = jnp.zeros((1, share), jnp.float32)
    outgoing = jnp.stack(
        [jnp.concatenate([blank_row, uppers[:-1]], 0), jnp.concatenate([lowers[1:], blank_row], 0)],
        1,
    )
    returned = lax.all_to_all(outgoing, GZ, split_axis=0, concat_axis=2, tiled=True)
    top_below = returned[0, 0].reshape(north_rows, NX)
    bottom_above = returned[0, 1].reshape(north_rows, NX)
    pressure_modes = local_part + spike * top_below + jnp.flip(spike, 0) * bottom_above
    back_sorted = jnp.einsum("zka,gxa->gxzk", pressure_modes, table_east, precision=HIGH).reshape(
        groups, east_rows, CZ * north_rows
    )
    returned_modes = lax.all_to_all(
        back_sorted, "xy", split_axis=0, concat_axis=0, tiled=True
    ).reshape(groups, east_rows, CZ, north_rows)
    pressure = jnp.einsum("gxzk,gky->xzy", returned_modes, table_north, precision=HIGH) * (
        1.0 / (NX * NY)
    )
    framed_pressure = extended(pressure, ((GZ, 1), ("xy", 0)), 1)
    pressure_west = framed_pressure[0, 1:-1]
    pressure_east = framed_pressure[-1, 1:-1]
    pressure_below = jnp.where(first_slab, 0.0, framed_pressure[1:-1, 0])
    pressure_above = framed_pressure[1:-1, -1]
    west_full = jnp.concatenate([pressure_west[None], pressure[:-1]], 0)
    east_full = jnp.concatenate([pressure[1:], pressure_east[None]], 0)
    below_full = jnp.concatenate([pressure_below[:, None], pressure[:, :-1]], 1)
    above_full = jnp.concatenate([pressure[:, 1:], pressure_above[:, None]], 1)
    open_east_after = fluid * jnp.concatenate([fluid[1:], fluid_east[None]], 0)
    open_north_after = jnp.roll(open_north, -1, 2)
    open_up_after = fluid * jnp.concatenate([fluid[:, 1:], fluid_above[:, None]], 1)
    applied = (
        open_east * (pressure - west_full)
        + open_east_after * (pressure - east_full)
        + open_north * (pressure - jnp.roll(pressure, 1, 2))
        + open_north_after * (pressure - jnp.roll(pressure, -1, 2))
        + open_up * (pressure - below_full)
        + open_up_after * (pressure - above_full)
    )
    residual = source - applied
    east_corrected = open_east * (east_velocity - (pressure - west_full))
    north_corrected = open_north * (north_velocity - (pressure - jnp.roll(pressure, 1, 2)))
    upward_corrected = open_up * (upward_velocity - (pressure - below_full))
    return (east_corrected, north_corrected, upward_corrected, pressure, residual)


def solution(mesh):
    torus = Mesh(mesh.devices.reshape(4, 4, 2, mesh.shape["xy"]), ("gz_0", "gz_1", "gz_2", "xy"))
    return jax.shard_map(
        local,
        mesh=torus,
        in_specs=(P("xy", GZ, None), P("xy", GZ, None), P("xy", GZ, None), P("xy", GZ, None)),
        out_specs=(
            P("xy", GZ, None),
            P("xy", GZ, None),
            P("xy", GZ, None),
            P("xy", GZ, None),
            P("xy", GZ, None),
        ),
        check_vma=False,
    )
```

profile of v0, /device:TPU:2, one launch (start us, length us, event | category | flops | bytes accessed | tf_op | source)
XLA Modules:
  0.0 263.1 jit_solution(14683449719377834362)
XLA Ops:
  6.4 3.6 %collective-permute-start.3 = (f32[3,64,1,512]{3,2,1,0:T(1,128)}, f32[3,64,1,512]{3,2,1,0:T(1,128)}, u32[]{:S(2)}, u32[]{:S(2)}) collective-permute-start(f32[3,64,1,512]{3,2,1,0:T(1,128)} %get-tuple-element.679), channel_id=1, source_target_pairs={{8,0},{16,8},{24,16},{32,24},{40,32},{48,40},{56,48},{64,56},{72,6... | collective-permute-start | bytes 1179656 | tf_op jit(solution)/shard_map/ppermute | solution.py:25
  10.0 4.2 %collective-permute-start.1 = (f32[3,1,8,512]{3,2,1,0:T(8,128)S(1)}, f32[3,1,8,512]{3,2,1,0:T(8,128)S(1)}, u32[]{:S(2)}, u32[]{:S(2)}) collective-permute-start(f32[3,1,8,512]{3,2,1,0:T(8,128)S(1)} %get-tuple-element.681), channel_id=1, source_target_pairs={{1,0},{2,1},{3,2},{4,3},{5,4},{6,5},{7,6},{0,7},{9,8},{10,9},{11,1... | collective-permute-start | bytes 147464 | tf_op jit(solution)/shard_map/ppermute | solution.py:25
  19.8 3.4 %fusion.77 = (f32[64,8,512]{2,1,0:T(8,128)S(1)}, f32[64,8,512]{2,1,0:T(8,128)S(1)}, f32[64,8,512]{2,1,0:T(8,128)S(1)}, f32[64,8,512]{2,1,0:T(8,128)S(1)}) fusion(f32[64,8,512]{2,1,0:T(8,128)} %param.14, f32[64,7,512]{2,1,0:T(8,128)} %get-tuple-element.694, f32[64,1,512]{2,1,0:T(1,128)S(1)} %fusion.54, s32[64,8,512]{2,1,0:T(8,128)S(1)} %copy-done.1, ...), kind=kLoop, calls=%fused_computation.146 | loop fusion | flops 2883584 | bytes 11534336 | tf_op jit(solution)/shard_map/mul | solution.py:144
  26.0 9.8 %fusion.30 = f32[8,64,64,8]{2,1,3,0:T(8,128)} fusion(f32[64,8,512]{2,1,0:T(8,128)S(1)} %fusion.20, s32[8,64]{1,0:T(8,128)S(1)} %copy-done.16), kind=kOutput, calls=%fused_computation.71 | convolution fusion | flops 1614544896 | bytes 2099200 | tf_op jit(solution)/shard_map/xzy,gky->gxzk/dot_general | solution.py:157
  35.8 3.1 %copy.26 = f32[8,64,512]{2,1,0:T(8,128)} copy(f32[8,64,512]{1,2,0:T(8,128)} %bitcast.158) | data formatting | bytes 2097152 | tf_op jit(solution)/shard_map/reshape | solution.py:157
  38.9 5.8 %all-to-all-start = ((f32[8,64,512]{2,1,0:T(8,128)}), f32[8,64,512]{2,1,0:T(8,128)}, u32[]{:S(2)}, u32[]{:S(2)}) async-start(f32[8,64,512]{2,1,0:T(8,128)} %copy.26), calls=%async_computation | async-start | bytes 2097152 | tf_op jit(solution)/shard_map/all_to_all | solution.py:160
  44.9 26.5 %all-to-all-done = f32[8,64,512]{2,1,0:T(8,128)} async-done(((f32[8,64,512]{2,1,0:T(8,128)}), f32[8,64,512]{2,1,0:T(8,128)}, u32[]{:S(2)}, u32[]{:S(2)}) %all-to-all-start) | async-done | bytes 1048608 | tf_op jit(solution)/shard_map/all_to_all | solution.py:160
  71.3 2.7 %reshape.211 = f32[8,64,8,64]{1,0,3,2:T(8,128)} reshape(f32[512,8,64]{0,2,1:T(8,128)} %bitcast.15) | data formatting | bytes 2097152 | tf_op jit(solution)/shard_map/reshape.46
  74.1 9.5 %fusion.7 = f32[8,1,64,512]{3,2,0,1:T(8,128)S(1)} fusion(f32[8,64,8,64]{1,0,3,2:T(8,128)} %reshape.211, s32[8,64]{1,0:T(8,128)S(1)} %copy-done.16), kind=kOutput, calls=%fused_computation.33 | convolution fusion | flops 1614544896 | bytes 2099200 | tf_op jit(solution)/shard_map/gxm,gxa->ma/dot_general | solution.py:161
  88.6 16.4 %while.71 = (s32[]{:T(128)}, f32[2,64,512]{2,1,0:T(8,128)S(1)}, f32[2,64,512]{2,1,0:T(8,128)S(1)}, f32[8,2,64,512]{3,2,1,0:T(8,128)}, f32[8,2,64,512]{3,2,1,0:T(...) while((s32[]{:T(128)}, f32[2,64,512]{2,1,0:T(8,128)S(1)}, ...), condition=%wide.region_1.2_spmd.clone, body=%wide.region_0.1_spmd.clone.sunk | while | flops 425987 | bytes 2100079 | solution.py:83
  88.7 2.0 bitcast_dynamic-update-slice_fusion.5
  90.7 2.0 bitcast_dynamic-update-slice_fusion.5
  98.9 2.0 bitcast_dynamic-update-slice_fusion.5
  101.0 2.0 bitcast_dynamic-update-slice_fusion.5
  103.0 2.0 bitcast_dynamic-update-slice_fusion.5
  106.6 15.6 %while.72 = (s32[]{:T(128)}, f32[2,64,512]{2,1,0:T(8,128)S(1)}, f32[8,2,64,512]{3,2,1,0:T(8,128)}, f32[8,2,64,512]{3,2,1,0:T(8,128)}, f32[8,2,64,512]{3,2,1,0:T(8,128)}, /*index=5*/s32[]{:T(128)}, s32[]{:T(128)}, s32[]{:T(128)}) while((s32[]{:T(128)}, f32[2,64,512]{2,1,0:T(8,128)S(1)}, f32[8,2,64,512]{3,2,1,0:T(8,128)}, ...), condition=%wide.region_3.4_spmd.clone, body=%wide.region_2.3_spmd.clone.sunk | while | flops 196612 | bytes 1310831 | solution.py:90
  124.1 3.9 %all_to_all.38 = f32[16,2,1,2,1024]{4,0,3,2,1:T(8,128)S(1)} all-to-all(f32[16,2,1,2,1024]{4,0,3,2,1:T(8,128)S(1)} %copy.32), channel_id=1, replica_groups=mesh['gz_0'=4,'gz_1'=4,'gz_2'=2,'xy'=8] {'gz_2'}, dimensions={1} | all-to-all | bytes 524288 | tf_op jit(solution)/shard_map/all_to_all | solution.py:51
  128.9 7.2 %all-to-all-start.2 = ((f32[16,2,1,2,1024]{4,1,3,2,0:T(2,128)}), f32[16,2,1,2,1024]{4,1,3,2,0:T(2,128)S(1)}, u32[]{:S(2)}, u32[]{:S(2)}) async-start(f32[16,2,1,2,1024]{4,1,3,2,0:T(2,128)} %copy.33), calls=%async_computation.2 | async-start | bytes 524288 | tf_op jit(solution)/shard_map/all_to_all | solution.py:51
  136.2 7.0 %all-to-all-done.2 = f32[16,2,1,2,1024]{4,1,3,2,0:T(2,128)S(1)} async-done(((f32[16,2,1,2,1024]{4,1,3,2,0:T(2,128)}), f32[16,2,1,2,1024]{4,1,3,2,0:T(2,128)S(1)}, u32[]{:S(2)}, u32[]{:S(2)}) %all-to-all-start.2) | async-done | bytes 262176 | tf_op jit(solution)/shard_map/all_to_all | solution.py:51
  143.6 10.0 %while.73 = (s32[]{:T(128)}, f32[1024]{0:T(1024)S(1)}, f32[1024]{0:T(1024)S(1)}, f32[32,1024]{1,0:T(8,128)S(1)}, f32[32,1024]{1,0:T(8,128)S(1)}, /*index=5*/f32[...) while((s32[]{:T(128)}, f32[1024]{0:T(1024)S(1)}, ...), condition=%wide.region_5.6_spmd.clone, body=%wide.region_4.5_spmd.clone.sunk | while | flops 17411 | bytes 86155 | solution.py:105
  153.7 10.4 %while.74 = (s32[]{:T(128)}, f32[1024]{0:T(1024)S(1)}, f32[32,1024]{1,0:T(8,128)S(1)}, f32[32,1024]{1,0:T(8,128)S(1)}, f32[32,1024]{1,0:T(8,128)S(1)}, /*index=5...) while((s32[]{:T(128)}, f32[1024]{0:T(1024)S(1)}, ...), condition=%wide.region_7.8_spmd.clone, body=%wide.region_6.7_spmd.clone.sunk | while | flops 14340 | bytes 86179 | solution.py:113
  165.2 16.9 %all-to-all-start.3 = ((f32[32,2,1024]{2,1,0:T(2,128)}), f32[32,2,1024]{2,1,0:T(2,128)S(1)}, u32[]{:S(2)}, u32[]{:S(2)}) async-start(f32[32,2,1024]{2,1,0:T(2,128)} %pad_maximum_fusion.5), calls=%async_computation.3 | async-start | bytes 524288 | tf_op jit(solution)/shard_map/all_to_all | solution.py:188
  183.4 6.4 %all-to-all-done.3 = f32[32,2,1024]{2,1,0:T(2,128)S(1)} async-done(((f32[32,2,1024]{2,1,0:T(2,128)}), f32[32,2,1024]{2,1,0:T(2,128)S(1)}, u32[]{:S(2)}, u32[]{:S(2)}) %all-to-all-start.3) | async-done | bytes 262176 | tf_op jit(solution)/shard_map/all_to_all | solution.py:188
  194.5 7.3 %fusion.34 = f32[8,64,512]{2,1,0:T(8,128)} fusion(f32[512,512,1]{1,0,2:T(8,128)S(1)} %bitcast.159, s32[8,64]{1,0:T(8,128)S(1)} %copy-done.17), kind=kOutput, calls=%fused_computation.75 | convolution fusion | flops 1614544896 | bytes 2099200 | tf_op jit(solution)/shard_map/zka,gxa->gxzk/dot_general | solution.py:192
  201.8 4.2 %all-to-all-start.4 = ((f32[8,64,512]{2,1,0:T(8,128)}), f32[8,64,512]{2,1,0:T(8,128)}, u32[]{:S(2)}, u32[]{:S(2)}) async-start(f32[8,64,512]{2,1,0:T(8,128)} %fusion.34), calls=%async_computation.4 | async-start | bytes 2097152 | tf_op jit(solution)/shard_map/all_to_all | solution.py:195
  209.5 26.1 %all-to-all-done.4 = f32[8,64,512]{2,1,0:T(8,128)} async-done(((f32[8,64,512]{2,1,0:T(8,128)}), f32[8,64,512]{2,1,0:T(8,128)}, u32[]{:S(2)}, u32[]{:S(2)}) %all-to-all-start.4) | async-done | bytes 1048608 | tf_op jit(solution)/shard_map/all_to_all | solution.py:195
  235.6 2.7 %reshape.213 = f32[8,64,8,64]{3,2,1,0:T(8,128)} reshape(f32[8,64,512]{2,1,0:T(8,128)} %all-to-all-done.4) | data formatting | bytes 2097152 | tf_op jit(solution)/shard_map/reshape | solution.py:197
  238.3 7.8 %fusion.10 = f32[64,8,512]{2,1,0:T(8,128)S(1)} fusion(f32[8,64,8,64]{3,2,1,0:T(8,128)} %reshape.213, s32[8,64]{1,0:T(8,128)} %multiply_add_fusion.1), kind=kOutput, calls=%fused_computation.35 | convolution fusion | flops 1614807040 | bytes 2099200 | tf_op jit(solution)/shard_map/gxzk,gky->xzy/dot_general | solution.py:198
  247.5 3.8 %collective-permute-start.7 = (f32[64,1,512]{2,1,0:T(1,128)S(1)}, f32[64,1,512]{2,1,0:T(1,128)S(1)}, u32[]{:S(2)}, u32[]{:S(2)}) collective-permute-start(f32[64,1,512]{2,1,0:T(1,128)S(1)} %get-tuple-element.691), channel_id=1, source_target_pairs={{8,0},{16,8},{24,16},{32,24},{40,32},{48,40},{56,48},{64,56},{72,6... | collective-permute-start | bytes 393224 | tf_op jit(solution)/shard_map/ppermute | solution.py:25
  251.8 2.9 %collective-permute-start.6 = (f32[1,8,512]{2,1,0:T(8,128)S(1)}, f32[1,8,512]{2,1,0:T(8,128)S(1)}, u32[]{:S(2)}, u32[]{:S(2)}) collective-permute-start(f32[1,8,512]{2,1,0:T(8,128)S(1)} %get-tuple-element.701), channel_id=1, source_target_pairs={{1,0},{2,1},{3,2},{4,3},{5,4},{6,5},{7,6},{0,7},{9,8},{10,9},{11,1... | collective-permute-start | bytes 49160 | tf_op jit(solution)/shard_map/ppermute | solution.py:25
  256.3 3.3 %subtract_multiply_fusion = (f32[64,8,512]{2,1,0:T(8,128)}, f32[64,8,512]{2,1,0:T(8,128)}, f32[64,8,512]{2,1,0:T(8,128)}) fusion(f32[64,8,512]{2,1,0:T(8,128)S(1)} %copy-done.3, f32[64,8,512]{2,1,0:T(8,128)S(1)} %fusion.10, f32[64,7,512]{2,1,0:T(8,128)S(1)} %get-tuple-element.690, f32[64,1,512]{2,1,0:T(1,128)S(1)} %broadcast_select_fusion.2, ...), kind=kLoop, calls=%fused_computation.78 | loop fusion | flops 4718592 | bytes 14680064 | tf_op jit(solution)/shard_map/mul | solution.py:224
  259.6 3.3 %fusion.27 = f32[64,8,512]{2,1,0:T(8,128)} fusion(f32[64,8,512]{2,1,0:T(8,128)S(1)} %copy-done.10, f32[1,8,512]{2,1,0:T(8,128)S(1)} %copy-done.14, f32[63,8,512]{2,1,0:T(8,128)S(1)} %copy-done.12, f32[64,8,512]{2,1,0:T(8,128)S(1)} %fusion.10, f32[1,8,512]{2,1,0:T(8,128)S(1)} %collective-permute-done.6, f32[63,8,512]{2,1,0:T(8,128)S(1)} %get-tuple-element.699, ...), kind=kLoop, calls=%fused_computation.63 | loop fusion | flops 9175040 | bytes 16777216 | tf_op jit(solution)/shard_map/sub | solution.py:221
  (456 shorter events, 76.5 us)
Async XLA Ops:
  0.6 1.7 copy-start.4
  0.6 1.8 copy-start.2
  3.8 14.9 %collective-permute-start.2 = (f32[3,64,1,512]{3,2,1,0:T(1,128)}, f32[3,64,1,512]{3,2,1,0:T(1,128)}, u32[]{:S(2)}, u32[]{:S(2)}) collective-permute-start(f32[3,64,1,512]{3,2,1,0:T(1,128)} %get-tuple-element.680), channel_id=1, source_target_pairs={{0,8},{8,16},{16,24},{24,32},{32,40},{40,48},{48,56},{56,64},{64,7... | collective-permute-start | bytes 1179656 | tf_op jit(solution)/shard_map/ppermute | solution.py:24
  4.5 13.6 %collective-permute-start = (f32[3,1,8,512]{3,2,1,0:T(8,128)}, f32[3,1,8,512]{3,2,1,0:T(8,128)S(1)}, u32[]{:S(2)}, u32[]{:S(2)}) collective-permute-start(f32[3,1,8,512]{3,2,1,0:T(8,128)} %get-tuple-element.682), channel_id=1, source_target_pairs={{0,1},{1,2},{2,3},{3,4},{4,5},{5,6},{6,7},{7,0},{8,9},{9,10},{10,1... | collective-permute-start | bytes 147464 | tf_op jit(solution)/shard_map/ppermute | solution.py:24
  6.4 17.4 %collective-permute-start.3 = (f32[3,64,1,512]{3,2,1,0:T(1,128)}, f32[3,64,1,512]{3,2,1,0:T(1,128)}, u32[]{:S(2)}, u32[]{:S(2)}) collective-permute-start(f32[3,64,1,512]{3,2,1,0:T(1,128)} %get-tuple-element.679), channel_id=1, source_target_pairs={{8,0},{16,8},{24,16},{32,24},{40,32},{48,40},{56,48},{64,56},{72,6... | collective-permute-start | bytes 1179656 | tf_op jit(solution)/shard_map/ppermute | solution.py:25
  10.0 8.2 %collective-permute-start.1 = (f32[3,1,8,512]{3,2,1,0:T(8,128)S(1)}, f32[3,1,8,512]{3,2,1,0:T(8,128)S(1)}, u32[]{:S(2)}, u32[]{:S(2)}) collective-permute-start(f32[3,1,8,512]{3,2,1,0:T(8,128)S(1)} %get-tuple-element.681), channel_id=1, source_target_pairs={{1,0},{2,1},{3,2},{4,3},{5,4},{6,5},{7,6},{0,7},{9,8},{10,9},{11,1... | collective-permute-start | bytes 147464 | tf_op jit(solution)/shard_map/ppermute | solution.py:25
  15.8 4.0 %copy-start.1 = (s32[64,8,512]{2,1,0:T(8,128)S(1)}, s32[64,8,512]{2,1,0:T(8,128)}, u32[]{:S(2)}) copy-start(s32[64,8,512]{2,1,0:T(8,128)} %param.15) | copy-start | bytes 3145732
  18.1 0.6 copy-start.15
  25.1 0.9 copy-start.16
  26.0 9.8 %copy-start.9 = (f32[64,8,512]{2,1,0:T(8,128)}, f32[64,8,512]{2,1,0:T(8,128)S(1)}, u32[]{:S(2)}) copy-start(f32[64,8,512]{2,1,0:T(8,128)S(1)} %fusion.20) | copy-start | bytes 3145732
  38.9 32.4 %all-to-all-start = ((f32[8,64,512]{2,1,0:T(8,128)}), f32[8,64,512]{2,1,0:T(8,128)}, u32[]{:S(2)}, u32[]{:S(2)}) async-start(f32[8,64,512]{2,1,0:T(8,128)} %copy.26), calls=%async_computation | async-start | bytes 2097152 | tf_op jit(solution)/shard_map/all_to_all | solution.py:160
  128.9 14.3 %all-to-all-start.2 = ((f32[16,2,1,2,1024]{4,1,3,2,0:T(2,128)}), f32[16,2,1,2,1024]{4,1,3,2,0:T(2,128)S(1)}, u32[]{:S(2)}, u32[]{:S(2)}) async-start(f32[16,2,1,2,1024]{4,1,3,2,0:T(2,128)} %copy.33), calls=%async_computation.2 | async-start | bytes 524288 | tf_op jit(solution)/shard_map/all_to_all | solution.py:51
  165.2 24.6 %all-to-all-start.3 = ((f32[32,2,1024]{2,1,0:T(2,128)}), f32[32,2,1024]{2,1,0:T(2,128)S(1)}, u32[]{:S(2)}, u32[]{:S(2)}) async-start(f32[32,2,1024]{2,1,0:T(2,128)} %pad_maximum_fusion.5), calls=%async_computation.3 | async-start | bytes 524288 | tf_op jit(solution)/shard_map/all_to_all | solution.py:188
  193.0 1.5 copy-start.17
  201.8 33.7 %all-to-all-start.4 = ((f32[8,64,512]{2,1,0:T(8,128)}), f32[8,64,512]{2,1,0:T(8,128)}, u32[]{:S(2)}, u32[]{:S(2)}) async-start(f32[8,64,512]{2,1,0:T(8,128)} %fusion.34), calls=%async_computation.4 | async-start | bytes 2097152 | tf_op jit(solution)/shard_map/all_to_all | solution.py:195
  246.2 13.4 %copy-start = (f32[64,8,512]{2,1,0:T(8,128)}, f32[64,8,512]{2,1,0:T(8,128)S(1)}, u32[]{:S(2)}) copy-start(f32[64,8,512]{2,1,0:T(8,128)S(1)} %fusion.10) | copy-start | bytes 3145732
  246.8 9.4 %copy-start.3 = (f32[64,8,512]{2,1,0:T(8,128)S(1)}, f32[64,8,512]{2,1,0:T(8,128)}, u32[]{:S(2)}) copy-start(f32[64,8,512]{2,1,0:T(8,128)} %param.14) | copy-start | bytes 3145732
  246.8 9.4 %copy-start.5 = (f32[64,8,512]{2,1,0:T(8,128)S(1)}, f32[64,8,512]{2,1,0:T(8,128)}, u32[]{:S(2)}) copy-start(f32[64,8,512]{2,1,0:T(8,128)} %param.12) | copy-start | bytes 3145732
  246.9 9.4 %copy-start.6 = (f32[64,7,512]{2,1,0:T(8,128)S(1)}, f32[64,7,512]{2,1,0:T(8,128)}, u32[]{:S(2)}) copy-start(f32[64,7,512]{2,1,0:T(8,128)} %get-tuple-element.694) | copy-start | bytes 2752516
  246.9 9.4 %copy-start.7 = (f32[63,8,512]{2,1,0:T(8,128)S(1)}, f32[63,8,512]{2,1,0:T(8,128)}, u32[]{:S(2)}) copy-start(f32[63,8,512]{2,1,0:T(8,128)} %get-tuple-element.704) | copy-start | bytes 3096580
  246.9 9.4 %copy-start.11 = (f32[64,8,512]{2,1,0:T(8,128)S(1)}, f32[64,8,512]{2,1,0:T(8,128)}, u32[]{:S(2)}) copy-start(f32[64,8,512]{2,1,0:T(8,128)} %param.13) | copy-start | bytes 3145732
  247.3 7.5 %collective-permute-start.5 = (f32[64,1,512]{2,1,0:T(1,128)S(1)}, f32[64,1,512]{2,1,0:T(1,128)S(1)}, u32[]{:S(2)}, u32[]{:S(2)}) collective-permute-start(f32[64,1,512]{2,1,0:T(1,128)S(1)} %get-tuple-element.692), channel_id=1, source_target_pairs={{0,8},{8,16},{16,24},{24,32},{32,40},{40,48},{48,56},{56,64},{64,7... | collective-permute-start | bytes 393224 | tf_op jit(solution)/shard_map/ppermute | solution.py:24
  247.5 12.1 %collective-permute-start.7 = (f32[64,1,512]{2,1,0:T(1,128)S(1)}, f32[64,1,512]{2,1,0:T(1,128)S(1)}, u32[]{:S(2)}, u32[]{:S(2)}) collective-permute-start(f32[64,1,512]{2,1,0:T(1,128)S(1)} %get-tuple-element.691), channel_id=1, source_target_pairs={{8,0},{16,8},{24,16},{32,24},{40,32},{48,40},{56,48},{64,56},{72,6... | collective-permute-start | bytes 393224 | tf_op jit(solution)/shard_map/ppermute | solution.py:25
  251.3 4.9 %collective-permute-start.4 = (f32[1,8,512]{2,1,0:T(8,128)S(1)}, f32[1,8,512]{2,1,0:T(8,128)S(1)}, u32[]{:S(2)}, u32[]{:S(2)}) collective-permute-start(f32[1,8,512]{2,1,0:T(8,128)S(1)} %get-tuple-element.702), channel_id=1, source_target_pairs={{0,1},{1,2},{2,3},{3,4},{4,5},{5,6},{6,7},{7,0},{8,9},{9,10},{10,1... | collective-permute-start | bytes 49160 | tf_op jit(solution)/shard_map/ppermute | solution.py:24
  251.8 7.8 %collective-permute-start.6 = (f32[1,8,512]{2,1,0:T(8,128)S(1)}, f32[1,8,512]{2,1,0:T(8,128)S(1)}, u32[]{:S(2)}, u32[]{:S(2)}) collective-permute-start(f32[1,8,512]{2,1,0:T(8,128)S(1)} %get-tuple-element.701), channel_id=1, source_target_pairs={{1,0},{2,1},{3,2},{4,3},{5,4},{6,5},{7,6},{0,7},{9,8},{10,9},{11,1... | collective-permute-start | bytes 49160 | tf_op jit(solution)/shard_map/ppermute | solution.py:25
  256.2 3.3 %copy-start.8 = (f32[64,7,512]{2,1,0:T(8,128)S(1)}, f32[64,7,512]{2,1,0:T(8,128)}, u32[]{:S(2)}) copy-start(f32[64,7,512]{2,1,0:T(8,128)} %get-tuple-element.693) | copy-start | bytes 2752516
  256.3 3.3 %copy-start.10 = (f32[64,8,512]{2,1,0:T(8,128)S(1)}, f32[64,8,512]{2,1,0:T(8,128)}, u32[]{:S(2)}) copy-start(f32[64,8,512]{2,1,0:T(8,128)} %copy-done.9) | copy-start | bytes 3145732
  256.3 3.3 %copy-start.12 = (f32[63,8,512]{2,1,0:T(8,128)S(1)}, f32[63,8,512]{2,1,0:T(8,128)}, u32[]{:S(2)}) copy-start(f32[63,8,512]{2,1,0:T(8,128)} %get-tuple-element.703) | copy-start | bytes 3096580
  256.3 3.3 %copy-start.13 = (f32[64,1,512]{2,1,0:T(1,128)S(1)}, f32[64,1,512]{2,1,0:T(1,128)}, u32[]{:S(2)}) copy-start(f32[64,1,512]{2,1,0:T(1,128)} %fusion.58) | copy-start | bytes 393220
  256.3 3.3 %copy-start.14 = (f32[1,8,512]{2,1,0:T(8,128)S(1)}, f32[1,8,512]{2,1,0:T(8,128)}, u32[]{:S(2)}) copy-start(f32[1,8,512]{2,1,0:T(8,128)} %slice_bitcast_fusion.4) | copy-start | bytes 49156
where the time goes:
time: 268 us; the launch traced here: 263 us
  waiting for transfers between devices  67.2 us (25%)
  other arithmetic  56.6 us (21%)
  starting transfers between devices  51.2 us (19%)
  local copies, waits for them, and re-layouts  44.5 us (17%)
  matrix products  34.4 us (13%)
  blocking collectives  3.94 us (1%)
  loops' own time  3.71 us (1%)
    dynamic_update_slice x16, other arithmetic, tridiagonal(): _, (ratios, values) = lax.scan(tridiagonal_forward, (start, start), right)  31.4 us
    all_to_all x1, waiting for transfers between devices, local(): lax.all_to_all(sorted_modes, 'xy', split_axis=0, concat_axis=0, tiled=True)  26.5 us
    all_to_all x1, waiting for transfers between devices, local(): lax.all_to_all(back_sorted, 'xy', split_axis=0, concat_axis=0, tiled=True)  26.1 us
    all_to_all x1, starting transfers between devices, local(): lax.all_to_all(outgoing, GZ, split_axis=0, concat_axis=2, tiled=True)  16.9 us
    ppermute x4, starting transfers between devices, extended(): lax.ppermute(initial, axis, [(b, a) for a, b in up])  14.5 us
    dynamic_update_slice x128, local copies, waits for them, and re-layouts, interface_chain(): lax.scan(interface_forward, (start, start), (bottoms, tops))  14.1 us
    dot_general x1, matrix products, local(): jnp.einsum('xzy,gky->gxzk', source, table_north, precision=HIGH)  9.77 us
    dot_general x1, matrix products, local(): jnp.einsum('gxm,gxa->ma', received, table_east, precision=HIGH)  9.49 us
  transfers between devices with their start and end apart: 12, of which 5 were waited for; matrix products, arithmetic and copies ran while one was open for 7% of the time, Pallas kernels for 0%

commit v1 on v0

v1 whole, which is shorter than its diff:
```python
import functools

import jax
import jax.numpy as jnp
import numpy as np
from jax import lax
from jax.experimental import pallas as pl
from jax.experimental.pallas import tpu as pltpu
from jax.sharding import PartitionSpec as P

NX = 512
NY = 512
NZ = 256
GZ = 32
XY = 8
XR = NX // XY
CZ = NZ // GZ
NH = 2
KL = NY // GZ // NH
XL = 128 // KL
J = XR // XL
LH = NY // NH
W = J * 128
ROWS = XR * CZ
F32 = jnp.float32
BF16 = jnp.bfloat16


def split(a):
    hi = a.astype(BF16)
    return hi, (a - hi.astype(F32)).astype(BF16)


def dot(a, b):
    return jnp.dot(a, b, preferred_element_type=F32)


def dot3(a, b):
    return dot(a[0], b[0]) + (dot(a[0], b[1]) + dot(a[1], b[0]))


def lanes(shape):
    return lax.broadcasted_iota(jnp.int32, shape, 1)


def roll(a, shift):
    return pltpu.roll(a, shift % 128, 1)


def exchange_lanes(tiles):
    tiles = list(tiles)
    group = lanes((8, 128)) // KL
    step = 1
    while step < XL:
        clear = (group & step) == 0
        for i in range(XL):
            if not i & step:
                k = i | step
                a, b = tiles[i], tiles[k]
                tiles[i] = jnp.where(clear, a, roll(b, step * KL))
                tiles[k] = jnp.where(clear, roll(a, -step * KL), b)
        step *= 2
    return tiles


def main_kernel(
    e_h, n_h, w_h, o_h, hh_h, hl_h, sh_h, sl_h, lam_h, mu_h, mup_h,
    p_v, f_v, src_v, zp_v, zf_v,
    e_v, n_v, w_v, o_v, hh, hl, sh, sl, lam, mu, mup,
    wa_v, zs_v, zps_v, y_v, send1, recv1, dh, dl, x_v, ea_v, eb_v, r_v, c_v, ag_v, uv_v, send2, recv2, zz_v,
    load_sem, halo_s, halo_r, a_s, a_r, g_s, g_r, b_s, b_r, ph_s, ph_r,
):
    me = lax.axis_index("gz")
    xi = lax.axis_index("xy")

    def gz(o):
        return {"gz": lax.rem(me + o, GZ)}

    def xy(o):
        return {"xy": lax.rem(xi + o, XY)}

    def load(k, src, dst):
        copy = pltpu.make_async_copy(src, dst, load_sem.at[k])
        copy.start()
        return copy

    def remote(src, dst, ssem, rsem, who):
        copy = pltpu.make_async_remote_copy(
            src_ref=src, dst_ref=dst, send_sem=ssem, recv_sem=rsem, device_id=who,
            device_id_type=pl.DeviceIdType.MESH,
        )
        copy.start()
        return copy

    loads = [
        load(0, o_h, o_v),
        load(1, w_h, w_v),
        load(2, e_h, e_v.at[pl.ds(0, ROWS)]),
        load(3, n_h, n_v),
        load(4, hh_h, hh),
        load(5, hl_h, hl),
        load(6, sh_h, sh),
        load(7, sl_h, sl),
        load(8, lam_h, lam),
        load(9, mu_h, mu),
        load(10, mup_h, mup),
    ]

    barrier = pltpu.get_barrier_semaphore()

    def greet_gz(o, _):
        pl.semaphore_signal(barrier, inc=1, device_id=gz(o), device_id_type=pl.DeviceIdType.MESH)
        return 0

    def greet_xy(o, _):
        pl.semaphore_signal(barrier, inc=1, device_id=xy(o), device_id_type=pl.DeviceIdType.MESH)
        return 0

    lax.fori_loop(1, GZ, greet_gz, 0)
    lax.fori_loop(1, XY, greet_xy, 0)

    loads[0].wait()

    def to_fluid(i, _):
        rows = pl.ds(pl.multiple_of(i * 64, 64), 64)
        f_v[pl.ds(pl.multiple_of(8 + i * 64, 8), 64), :] = (1 - o_v[rows, :]).astype(F32)
        return 0

    lax.fori_loop(0, ROWS // 64, to_fluid, 0)
    loads[1].wait()
    loads[2].wait()

    def edge(i, _):
        for k in range(8):
            x = i * 8 + k
            zs_v[pl.ds(x, 1), :] = f_v[pl.ds(x * 8 + 15, 1), :]
            zs_v[pl.ds(XR + x, 1), :] = f_v[pl.ds(x * 8 + 8, 1), :]
            zs_v[pl.ds(2 * XR + x, 1), :] = w_v[pl.ds(x * 8, 1), :]
        return 0

    lax.fori_loop(0, XR // 8, edge, 0)
    pl.semaphore_wait(barrier, GZ - 1 + XY - 1)
    halos = [
        remote(zs_v.at[pl.ds(2 * XR, XR)], wa_v, halo_s.at[0], halo_r.at[0], gz(GZ - 1)),
        remote(zs_v.at[pl.ds(XR, XR)], zf_v.at[pl.ds(XR, XR)], halo_s.at[1], halo_r.at[1], gz(GZ - 1)),
        remote(zs_v.at[pl.ds(0, XR)], zf_v.at[pl.ds(0, XR)], halo_s.at[2], halo_r.at[2], gz(1)),
        remote(f_v.at[pl.ds(ROWS, 8)], f_v.at[pl.ds(0, 8)], halo_s.at[3], halo_r.at[3], xy(1)),
        remote(f_v.at[pl.ds(8, 8)], f_v.at[pl.ds(ROWS + 8, 8)], halo_s.at[4], halo_r.at[4], xy(XY - 1)),
        remote(e_v.at[pl.ds(0, 8)], e_v.at[pl.ds(ROWS, 8)], halo_s.at[5], halo_r.at[5], xy(XY - 1)),
    ]
    loads[3].wait()
    for k in range(4, 11):
        loads[k].wait()
    for h in halos:
        h.wait()

    sub = lax.broadcasted_iota(jnp.int32, (8, NY), 0)
    first = me == 0
    last = me == GZ - 1

    def source(i, _):
        base = pl.multiple_of(i * 8, 8)
        here = pl.ds(base, 8)
        f = f_v[pl.ds(pl.multiple_of(base + 8, 8), 8), :]
        fw = f_v[here, :]
        fe = f_v[pl.ds(pl.multiple_of(base + 16, 8), 8), :]
        east = f * (fw * e_v[here, :] - fe * e_v[pl.ds(pl.multiple_of(base + 8, 8), 8), :])
        fn = f * pltpu.roll(f, 1, 1) * n_v[here, :]
        north = fn - pltpu.roll(fn, NY - 1, 1)
        w = w_v[here, :]
        below = jnp.broadcast_to(zf_v[pl.ds(i, 1), :], (8, NY))
        above = jnp.broadcast_to(zf_v[pl.ds(XR + i, 1), :], (8, NY))
        wabove = jnp.broadcast_to(wa_v[pl.ds(i, 1), :], (8, NY))
        below = jnp.where(first, 1.0, below)
        above = jnp.where(last, 0.0, above)
        fb = jnp.where(sub == 0, below, pltpu.roll(f, 1, 0))
        fa = jnp.where(sub == 7, above, pltpu.roll(f, 7, 0))
        wn = jnp.where(sub == 7, wabove, pltpu.roll(w, 7, 0))
        up = f * (fb * w - fa * wn)
        src_v[here, :] = east + north + up
        return 0

    lax.fori_loop(0, XR, source, 0)

    def wait_bytes(ref, sem):
        pltpu.make_async_copy(ref, ref, sem).wait()

    for h in range(NH):
        hcol = pl.ds(h * LH, LH)

        def forward(i, _):
            rows = pl.ds(pl.multiple_of(i * 256, 256), 256)
            y_v[rows, :] = dot3(split(src_v[rows, :]), (hh[:, hcol], hl[:, hcol]))
            return 0

        lax.fori_loop(0, ROWS // 256, forward, 0)

        def pack(j, _):
            for t in range(LH // 128):
                tiles = exchange_lanes(
                    [y_v[pl.ds(pl.multiple_of((x * J + j) * 8, 8), 8), pl.ds(t * 128, 128)] for x in range(XL)]
                )
                for a in range(XL):
                    send1[pl.ds((h * GZ + t * XL + a) * 8, 8), pl.ds(pl.multiple_of(j * 128, 128), 128)] = tiles[a]
            return 0

        lax.fori_loop(0, J, pack, 0)

        mine = pl.ds(pl.multiple_of(h * NZ + me * 8, 8), 8)

        def go(o, _):
            to = lax.rem(me + o, GZ)
            remote(
                send1.at[pl.ds(pl.multiple_of((h * GZ + to) * 8, 8), 8)], recv1.at[mine],
                a_s.at[h], a_r.at[h], {"gz": to},
            )
            return 0

        lax.fori_loop(1, GZ, go, 0)
        recv1[mine, :] = send1[pl.ds(pl.multiple_of((h * GZ + me) * 8, 8), 8), :]

    for h in range(NH):
        lrow = lam[pl.ds(h * GZ + me, 1), :]

        def rates(i, _):
            rows = pl.ds(pl.multiple_of(i * 16, 16), 16)
            out = pl.ds(pl.multiple_of(h * NZ + i * 16, 16), 16)
            g = mu[rows, :] + lrow
            root = jnp.sqrt(g + 0.25 * g * g)
            r_v[out, :] = 1.0 / (1.0 + 0.5 * g + root)
            c_v[out, :] = (1.0 / (NZ + 1) / NY) / root
            return 0

        lax.fori_loop(0, NZ // 16, rates, 0)

    group = lanes((16, 128)) // KL

    def squares(r):
        out = [r]
        for _ in range(5):
            out.append(out[-1] * out[-1])
        return out

    LOGJ = J.bit_length() - 1
    LOGX = XL.bit_length() - 1

    for h in range(NH):
        wait_bytes(recv1.at[pl.ds(h * NZ, NZ - 8)], a_r.at[h])

        def cut(i, _):
            rows = pl.ds(pl.multiple_of(i * 16, 16), 16)
            a, b = split(recv1[pl.ds(pl.multiple_of(h * NZ + i * 16, 16), 16), :])
            dh[rows, :] = a
            dl[rows, :] = b
            return 0

        lax.fori_loop(0, NZ // 16, cut, 0)
        for c in range(W // 256):
            col = pl.ds(c * 256, 256)
            x_v[pl.ds(h * NZ, NZ), col] = dot3((sh[...], sl[...]), (dh[:, col], dl[:, col]))

        def sums(q, carry):
            pa, pb = carry
            rows = pl.ds(pl.multiple_of(h * NZ + q * 16, 16), 16)
            r = r_v[rows, :]
            s = [x_v[rows, pl.ds(j * 128, 128)] for j in range(J)]
            u = [s[0]]
            for j in range(1, J):
                u.append(s[j] + r * u[-1])
            v = [s[-1]]
            for j in range(J - 2, -1, -1):
                v.append(s[j] + r * v[-1])
            v = v[::-1]
            for j in range(J):
                x_v[rows, pl.ds(j * 128, 128)] = u[j] + v[j] - s[j]
            a, b = u[-1], v[0]
            pw = r
            for _ in range(LOGJ):
                pw = pw * pw
            step = 1
            while step < XL:
                a = a + jnp.where(group >= step, pw * roll(a, step * KL), 0.0)
                b = b + jnp.where(group < XL - step, pw * roll(b, -step * KL), 0.0)
                pw = pw * pw
                step *= 2
            ea_v[rows, :] = jnp.where(group >= 1, roll(a, KL), 0.0)
            eb_v[rows, :] = jnp.where(group < XL - 1, roll(b, -KL), 0.0)
            at = group == q
            pa = jnp.where(at, pltpu.roll(a, lax.rem((q + 1) * KL, 128), 1), pa)
            pb = jnp.where(at, pltpu.roll(b, q * KL, 1), pb)
            return pa, pb

        zero = jnp.zeros((16, 128), F32)
        pa, pb = lax.fori_loop(0, NZ // 16, sums, (zero, zero))
        own = pl.ds(pl.multiple_of((h * XY + xi) * 32, 32), 32)
        ag_v[pl.ds(pl.multiple_of((h * XY + xi) * 32, 32), 16), :] = pa
        ag_v[pl.ds(pl.multiple_of((h * XY + xi) * 32 + 16, 16), 16), :] = pb

        def spread(o, _):
            remote(ag_v.at[own], ag_v.at[own], g_s.at[h], g_r.at[h], xy(o))
            return 0

        lax.fori_loop(1, XY, spread, 0)

    for h in range(NH):
        wait_bytes(ag_v.at[pl.ds(h * XY * 32, (XY - 1) * 32)], g_r.at[h])
        g = mup[...] + lam[pl.ds(h * GZ + me, 1), :]
        rp = 1.0 / (1.0 + 0.5 * g + jnp.sqrt(g + 0.25 * g * g))
        for _ in range(XR.bit_length() - 1):
            rp = rp * rp
        full = rp
        for _ in range(XY.bit_length() - 1):
            full = full * full
        close = 1.0 / (1.0 - full)

        def piece(o, part):
            at = (h * XY + lax.rem(xi + o, XY)) * 32 + part * 16
            return ag_v[pl.ds(pl.multiple_of(at, 16), 16), :]

        un, vn = piece(0, 0), piece(0, 1)
        for o in range(1, XY):
            un = un * rp + piece(o, 0)
            vn = vn * rp + piece(XY - o, 1)
        un = un * close
        vn = vn * close

        def finish(q, _):
            rows = pl.ds(pl.multiple_of(h * NZ + q * 16, 16), 16)
            out = pl.ds(pl.multiple_of(q * 16, 16), 16)
            at = group == q
            ub = jnp.where(at, un, 0.0)
            vb = jnp.where(at, vn, 0.0)
            step = 1
            while step < XL:
                ub = ub + roll(ub, step * KL)
                vb = vb + roll(vb, step * KL)
                step *= 2
            r = r_v[rows, :]
            powers = [r]
            for _ in range(J - 1):
                powers.append(powers[-1] * r)
            pw = powers[-1]
            up = jnp.ones_like(r)
            down = jnp.ones_like(r)
            step = 1
            while step < XL:
                on = (group & step) != 0
                up = jnp.where(on, up * pw, up)
                down = jnp.where(on, down, down * pw)
                pw = pw * pw
                step *= 2
            cu = ea_v[rows, :] + up * ub
            cv = eb_v[rows, :] + down * vb
            c = c_v[rows, :]
            for j in range(J):
                col = pl.ds(j * 128, 128)
                sol = c * (x_v[rows, col] + powers[j] * cu + powers[J - 1 - j] * cv)
                a, b = split(sol)
                dh[out, col] = a
                dl[out, col] = b
            return 0

        lax.fori_loop(0, NZ // 16, finish, 0)
        for c in range(W // 256):
            col = pl.ds(c * 256, 256)
            send2[pl.ds(h * NZ, NZ), col] = dot3((sh[...], sl[...]), (dh[:, col], dl[:, col]))

        mine = pl.ds(pl.multiple_of((h * GZ + me) * 8, 8), 8)

        def back(o, _):
            to = lax.rem(me + o, GZ)
            remote(
                send2.at[pl.ds(pl.multiple_of(h * NZ + to * 8, 8), 8)], recv2.at[mine],
                b_s.at[h], b_r.at[h], {"gz": to},
            )
            return 0

        lax.fori_loop(1, GZ, back, 0)
        recv2[mine, :] = send2[pl.ds(pl.multiple_of(h * NZ + me * 8, 8), 8), :]

    for h in range(NH):
        wait_bytes(recv2.at[pl.ds(h * NZ, NZ - 8)], b_r.at[h])

        def unpack(j, _):
            for t in range(LH // 128):
                tiles = exchange_lanes(
                    [
                        recv2[pl.ds((h * GZ + t * XL + a) * 8, 8), pl.ds(pl.multiple_of(j * 128, 128), 128)]
                        for a in range(XL)
                    ]
                )
                for x in range(XL):
                    zz_v[pl.ds(pl.multiple_of((x * J + j) * 8, 8), 8), pl.ds(t * 128, 128)] = tiles[x]
            return 0

        lax.fori_loop(0, J, unpack, 0)

        def inverse(i, _):
            rows = pl.ds(pl.multiple_of(i * 256, 256), 256)
            out = pl.ds(pl.multiple_of(8 + i * 256, 8), 256)
            hrow = pl.ds(h * LH, LH)
            part = dot3(split(zz_v[rows, :]), (hh[hrow, :], hl[hrow, :]))
            p_v[out, :] = part if h == 0 else p_v[out, :] + part
            return 0

        lax.fori_loop(0, ROWS // 256, inverse, 0)

    def pedge(i, _):
        for k in range(8):
            x = i * 8 + k
            zps_v[pl.ds(x, 1), :] = p_v[pl.ds(x * 8 + 15, 1), :]
            zps_v[pl.ds(XR + x, 1), :] = p_v[pl.ds(x * 8 + 8, 1), :]
        return 0

    lax.fori_loop(0, XR // 8, pedge, 0)
    planes = [
        remote(zps_v.at[pl.ds(0, XR)], zp_v.at[pl.ds(0, XR)], ph_s.at[0], ph_r.at[0], gz(1)),
        remote(zps_v.at[pl.ds(XR, XR)], zp_v.at[pl.ds(XR, XR)], ph_s.at[1], ph_r.at[1], gz(GZ - 1)),
        remote(p_v.at[pl.ds(ROWS, 8)], p_v.at[pl.ds(0, 8)], ph_s.at[2], ph_r.at[2], xy(1)),
        remote(p_v.at[pl.ds(8, 8)], p_v.at[pl.ds(ROWS + 8, 8)], ph_s.at[3], ph_r.at[3], xy(XY - 1)),
    ]
    for h in range(NH):
        wait_bytes(send1.at[pl.ds(h * NZ, NZ - 8)], a_s.at[h])
        wait_bytes(ag_v.at[pl.ds(h * XY * 32, (XY - 1) * 32)], g_s.at[h])
        wait_bytes(send2.at[pl.ds(h * NZ, NZ - 8)], b_s.at[h])
    for c in planes:
        c.wait()


def last_kernel(e, n, w, src, p_v, f_v, zp, zf, eo, no, wo, po, ro):
    step = pl.program_id(0)
    me = lax.axis_index("gz")
    first = me == 0
    last = me == GZ - 1
    sub = lax.broadcasted_iota(jnp.int32, (8, NY), 0)

    def one(i, _):
        here = pl.ds(pl.multiple_of(i * 8, 8), 8)
        x = step * 8 + i
        base = pl.multiple_of(x * 8, 8)
        mid = pl.ds(pl.multiple_of(base + 8, 8), 8)
        east = pl.ds(pl.multiple_of(base + 16, 8), 8)
        p = p_v[mid, :]
        f = f_v[mid, :]
        below = jnp.where(first, 1.0, jnp.broadcast_to(zf[pl.ds(x, 1), :], (8, NY)))
        above = jnp.where(last, 0.0, jnp.broadcast_to(zf[pl.ds(XR + x, 1), :], (8, NY)))
        pbelow = jnp.where(first, 0.0, jnp.broadcast_to(zp[pl.ds(x, 1), :], (8, NY)))
        pabove = jnp.broadcast_to(zp[pl.ds(XR + x, 1), :], (8, NY))
        oe = f * f_v[pl.ds(base, 8), :]
        oe_next = f * f_v[east, :]
        on = f * pltpu.roll(f, 1, 1)
        on_next = pltpu.roll(on, NY - 1, 1)
        ou = f * jnp.where(sub == 0, below, pltpu.roll(f, 1, 0))
        ou_next = f * jnp.where(sub == 7, above, pltpu.roll(f, 7, 0))
        de = p - p_v[pl.ds(base, 8), :]
        de_next = p - p_v[east, :]
        dn = p - pltpu.roll(p, 1, 1)
        dn_next = p - pltpu.roll(p, NY - 1, 1)
        du = p - jnp.where(sub == 0, pbelow, pltpu.roll(p, 1, 0))
        du_next = p - jnp.where(sub == 7, pabove, pltpu.roll(p, 7, 0))
        applied = oe * de + oe_next * de_next + on * dn + on_next * dn_next + ou * du + ou_next * du_next
        ro[here, :] = src[here, :] - applied
        eo[here, :] = oe * (e[here, :] - de)
        no[here, :] = on * (n[here, :] - dn)
        wo[here, :] = ou * (w[here, :] - du)
        po[here, :] = p
        return 0

    lax.fori_loop(0, 8, one, 0)


def tables():
    i = np.arange(NY)
    angle = 2 * np.pi * ((i[:, None] * i[None, :]) % NY) / NY
    hart = np.cos(angle) + np.sin(angle)
    k = np.arange(1, NZ + 1)
    sine = np.sin(np.pi * ((k[:, None] * k[None, :]) % (2 * (NZ + 1))) / (NZ + 1))
    lam = 4 * np.sin(np.pi * i / NY) ** 2
    mu = 4 * np.sin(np.pi * k / (2 * (NZ + 1))) ** 2

    def cut(a):
        hi = a.astype(np.float32).astype(BF16)
        return hi, (a - hi.astype(np.float64)).astype(np.float32).astype(BF16)

    lanes_of = np.arange(128)
    half = np.arange(NH)[:, None, None]
    who = np.arange(GZ)[None, :, None]
    lam = lam[half * LH + who * KL + lanes_of[None, None, :] % KL].reshape(NH * GZ, 128)
    packed = mu[(lanes_of[None, :] // KL) * 16 + np.arange(16)[:, None]]
    mu = np.repeat(mu[:, None], 128, 1)
    return (*cut(hart), *cut(sine), lam.astype(np.float32), mu.astype(np.float32), packed.astype(np.float32))


def local(east_velocity, north_velocity, upward_velocity, obstacle):
    e, n, w, o = (a.reshape(ROWS, NY) for a in (east_velocity, north_velocity, upward_velocity, obstacle))
    consts = [jnp.asarray(t) for t in tables()]
    any_spec = pl.BlockSpec(memory_space=pl.ANY)
    vmem = pl.BlockSpec(memory_space=pltpu.VMEM)
    ext = jax.ShapeDtypeStruct((ROWS + 16, NY), F32)
    planes = jax.ShapeDtypeStruct((2 * XR, NY), F32)

    def v(*shape, dtype=F32):
        return pltpu.VMEM(shape, dtype)

    dma = pltpu.SemaphoreType.DMA
    p, f, src, zp, zf = pl.pallas_call(
        main_kernel,
        out_shape=[ext, ext, jax.ShapeDtypeStruct((ROWS, NY), F32), planes, planes],
        in_specs=[any_spec] * 11,
        out_specs=[vmem] * 5,
        scratch_shapes=[
            v(ROWS + 8, NY), v(ROWS, NY), v(ROWS, NY), v(ROWS, NY, dtype=jnp.int32),
            v(NY, NY, dtype=BF16), v(NY, NY, dtype=BF16), v(NZ, NZ, dtype=BF16), v(NZ, NZ, dtype=BF16),
            v(NH * GZ, 128), v(NZ, 128), v(16, 128),
            v(XR, NY), v(3 * XR, NY), v(2 * XR, NY),
            v(ROWS, LH), v(NH * NZ, W), v(NH * NZ, W), v(NZ, W, dtype=BF16), v(NZ, W, dtype=BF16),
            v(NH * NZ, W), v(NH * NZ, 128), v(NH * NZ, 128), v(NH * NZ, 128), v(NH * NZ, 128),
            v(NH * XY * 32, 128), v(32, 128), v(NH * NZ, W), v(NH * NZ, W), v(ROWS, LH),
            dma((11,)), dma((6,)), dma((6,)), dma((NH,)), dma((NH,)), dma((NH,)), dma((NH,)),
            dma((NH,)), dma((NH,)), dma((4,)), dma((4,)),
        ],
        compiler_params=pltpu.CompilerParams(
            collective_id=0, has_side_effects=True, vmem_limit_bytes=40 * 1024 * 1024
        ),
        name="main",
    )(e, n, w, o, *consts)

    block = pl.BlockSpec((64, NY), lambda i: (i, 0))
    out = jax.ShapeDtypeStruct((ROWS, NY), F32)
    outs = pl.pallas_call(
        last_kernel,
        grid=(ROWS // 64,),
        out_shape=[out] * 5,
        in_specs=[block] * 4 + [pl.BlockSpec(a.shape, lambda i: (0, 0)) for a in (p, f, zp, zf)],
        out_specs=[block] * 5,
        compiler_params=pltpu.CompilerParams(vmem_limit_bytes=24 * 1024 * 1024),
        name="last",
    )(e, n, w, src, p, f, zp, zf)
    return tuple(a.reshape(XR, CZ, NY) for a in outs)


def solution(mesh):
    spec = P("xy", "gz", None)
    return jax.shard_map(local, mesh=mesh, in_specs=(spec,) * 4, out_specs=(spec,) * 5, check_vma=False)
```

time: 268 us -> 103 us (0.38); the launches traced: 263 us -> 102 us
  Pallas kernels: 0 us -> 90.4 us
  waiting for transfers between devices: 67.2 us -> 0 us
  other arithmetic: 56.6 us -> 0 us
  starting transfers between devices: 51.2 us -> 0 us
  matrix products: 34.4 us -> 0 us
  local copies, waits for them, and re-layouts: 44.5 us -> 11.1 us
  blocking collectives: 3.94 us -> 0 us
  loops' own time: 3.71 us -> 0 us
    pallas_call x0 -> x2, Pallas kernels: none -> 90.4 us  [the longest x1 79.8 us: local(): pl.pallas_call(main_kernel, out_shape=[ext, ext, jax.ShapeDtypeStruct((RO...]
    all_to_all x4 -> x0, waiting for transfers between devices: 65.9 us -> none  [the longest x1 26.5 us: local(): lax.all_to_all(sorted_modes, 'xy', split_axis=0, concat_axis=0, tiled=True)]
    dot_general x4 -> x0, matrix products: 34.4 us -> none  [the longest x1 9.77 us: local(): jnp.einsum('xzy,gky->gxzk', source, table_north, precision=HIGH)]
    all_to_all x4 -> x0, starting transfers between devices: 34.1 us -> none  [the longest x1 16.9 us: local(): lax.all_to_all(outgoing, GZ, split_axis=0, concat_axis=2, tiled=True)]
    dynamic_update_slice x16 -> x0, other arithmetic: 31.4 us -> none  [tridiagonal(): _, (ratios, values) = lax.scan(tridiagonal_forward, (start, start), right)]
    ppermute x8 -> x0, starting transfers between devices: 17.1 us -> none  [the longest x4 14.5 us: extended(): lax.ppermute(initial, axis, [(b, a) for a, b in up])]
    dynamic_update_slice x128 -> x0, local copies, waits for them, and re-layouts: 14.1 us -> none  [interface_chain(): lax.scan(interface_forward, (start, start), (bottoms, tops))]
    unnamed x40 -> x22, local copies, waits for them, and re-layouts: 2.11 us -> 11.1 us
  transfers between devices with their start and end apart: 12 -> 0, of which waited for: 5 -> 0; matrix products, arithmetic and copies ran while one was open for 7% -> 0% of each run, Pallas kernels for 0% -> 0%
where the time goes in v1:
time: 103 us; the launch traced here: 102 us
  Pallas kernels  90.4 us (88%)
  local copies, waits for them, and re-layouts  11.1 us (11%)
    pallas_call x1, Pallas kernels, local(): pl.pallas_call(main_kernel, out_shape=[ext, ext, jax.ShapeDtypeStruct((RO...  79.8 us
    unnamed x22, local copies, waits for them, and re-layouts  11.1 us
    pallas_call x1, Pallas kernels, local(): pl.pallas_call(last_kernel, grid=(ROWS // 64,), out_shape=[out] * 5, in_s...  10.6 us

profile of v1, /device:TPU:2, one launch (start us, length us, event | category | flops | bytes accessed | tf_op | source)
XLA Modules:
  0.0 102.2 jit_solution(17325346981630411731)
XLA Ops:
  0.6 0.0 copy-start
  0.6 1.2 %copy-done = f32[64,8,512]{2,1,0:T(8,128)S(1)} copy-done((f32[64,8,512]{2,1,0:T(8,128)S(1)}, f32[64,8,512]{2,1,0:T(8,128)}, u32[]{:S(2)}) %copy-start) | copy-done | bytes 1048600
  1.9 0.0 copy-start.1
  1.9 1.2 %copy-done.1 = f32[64,8,512]{2,1,0:T(8,128)S(1)} copy-done((f32[64,8,512]{2,1,0:T(8,128)S(1)}, f32[64,8,512]{2,1,0:T(8,128)}, u32[]{:S(2)}) %copy-start.1) | copy-done | bytes 1048600
  3.1 0.0 copy-start.2
  3.1 1.2 %copy-done.2 = f32[64,8,512]{2,1,0:T(8,128)S(1)} copy-done((f32[64,8,512]{2,1,0:T(8,128)S(1)}, f32[64,8,512]{2,1,0:T(8,128)}, u32[]{:S(2)}) %copy-start.2) | copy-done | bytes 1048600
  4.3 0.0 copy-start.3
  4.3 1.2 %copy-done.3 = s32[64,8,512]{2,1,0:T(8,128)S(1)} copy-done((s32[64,8,512]{2,1,0:T(8,128)S(1)}, s32[64,8,512]{2,1,0:T(8,128)}, u32[]{:S(2)}) %copy-start.3) | copy-done | bytes 1048600
  5.5 0.0 copy-start.4
  5.5 1.0 %copy-done.4 = bf16[512,512]{1,0:T(8,128)(2,1)S(1)} copy-done((bf16[512,512]{1,0:T(8,128)(2,1)S(1)}, bf16[512,512]{1,0:T(8,128)(2,1)}, u32[]{:S(2)}) %copy-start.4) | copy-done | bytes 524312
  6.6 0.0 copy-start.5
  6.6 1.0 %copy-done.5 = bf16[512,512]{1,0:T(8,128)(2,1)S(1)} copy-done((bf16[512,512]{1,0:T(8,128)(2,1)S(1)}, bf16[512,512]{1,0:T(8,128)(2,1)}, u32[]{:S(2)}) %copy-start.5) | copy-done | bytes 524312
  7.6 0.0 copy-start.6
  7.6 0.9 copy-done.6
  8.5 0.0 copy-start.7
  8.5 0.9 copy-done.7
  9.4 0.0 copy-start.8
  9.4 0.9 copy-done.8
  10.3 0.0 copy-start.9
  10.3 0.8 copy-done.9
  11.1 0.0 copy-start.10
  11.1 0.7 copy-done.10
  11.8 79.8 %main.1 = (f32[528,512]{1,0:T(8,128)S(1)}, f32[528,512]{1,0:T(8,128)S(1)}, f32[512,512]{1,0:T(8,128)S(1)}, f32[128,512]{1,0:T(8,128)S(1)}, f32[128,512]{1,0:T(8,128)S(1)}) custom-call(f32[512,512]{1,0:T(8,128)S(1)} %bitcast.9, f32[512,512]{1,0:T(8,128)S(1)} %bitcast.11, f32[512,512]{1,0:T(8,128)S(1)} %bitcast.13, s32[512,512]{1,0:T(8,128)S(1)} %bitcast.15, ...), custom_call_target="tpu_custom_call" | custom-call | tf_op jit(solution)/shard_map/main/pallas_call | solution.py:506
  91.6 10.6 %last.1 = (f32[512,512]{1,0:T(8,128)}, f32[512,512]{1,0:T(8,128)}, f32[512,512]{1,0:T(8,128)}, f32[512,512]{1,0:T(8,128)}, f32[512,512]{1,0:T(8,128)}) custom-call(f32[512,512]{1,0:T(8,128)S(1)} %bitcast.10, f32[512,512]{1,0:T(8,128)S(1)} %bitcast.12, f32[512,512]{1,0:T(8,128)S(1)} %bitcast.14, f32[512,512]{1,0:T(8,128)S(1)} %get-tuple-element.15.src, ...), custom_call_target="tpu_custom_call" | custom-call | tf_op jit(solution)/shard_map/last/pallas_call | solution.py:530
Async XLA Ops:
  0.6 1.2 %copy-start = (f32[64,8,512]{2,1,0:T(8,128)S(1)}, f32[64,8,512]{2,1,0:T(8,128)}, u32[]{:S(2)}) copy-start(f32[64,8,512]{2,1,0:T(8,128)} %param.11) | copy-start | bytes 3145732
  1.9 1.2 %copy-start.1 = (f32[64,8,512]{2,1,0:T(8,128)S(1)}, f32[64,8,512]{2,1,0:T(8,128)}, u32[]{:S(2)}) copy-start(f32[64,8,512]{2,1,0:T(8,128)} %param.12) | copy-start | bytes 3145732
  3.1 1.2 %copy-start.2 = (f32[64,8,512]{2,1,0:T(8,128)S(1)}, f32[64,8,512]{2,1,0:T(8,128)}, u32[]{:S(2)}) copy-start(f32[64,8,512]{2,1,0:T(8,128)} %param.13) | copy-start | bytes 3145732
  4.3 1.2 %copy-start.3 = (s32[64,8,512]{2,1,0:T(8,128)S(1)}, s32[64,8,512]{2,1,0:T(8,128)}, u32[]{:S(2)}) copy-start(s32[64,8,512]{2,1,0:T(8,128)} %param.14) | copy-start | bytes 3145732
  5.5 1.0 %copy-start.4 = (bf16[512,512]{1,0:T(8,128)(2,1)S(1)}, bf16[512,512]{1,0:T(8,128)(2,1)}, u32[]{:S(2)}) copy-start(bf16[512,512]{1,0:T(8,128)(2,1)} %constant.15.clone.hl_h) | copy-start | bytes 1572868
  6.6 1.0 %copy-start.5 = (bf16[512,512]{1,0:T(8,128)(2,1)S(1)}, bf16[512,512]{1,0:T(8,128)(2,1)}, u32[]{:S(2)}) copy-start(bf16[512,512]{1,0:T(8,128)(2,1)} %constant.14.clone.hh_h) | copy-start | bytes 1572868
  7.6 0.9 copy-start.6
  8.5 0.9 copy-start.7
  9.4 0.9 copy-start.8
  10.3 0.8 copy-start.9
  11.1 0.7 copy-start.10

commit v2 on v1

v2 whole, which is shorter than its diff:
```python
import functools

import jax
import jax.numpy as jnp
import numpy as np
from jax import lax
from jax.experimental import pallas as pl
from jax.experimental.pallas import tpu as pltpu
from jax.sharding import PartitionSpec as P

NX = 512
NY = 512
NZ = 256
GZ = 32
XY = 8
XR = NX // XY
CZ = NZ // GZ
NH = 2
KL = NY // GZ // NH
XL = 128 // KL
J = XR // XL
LH = NY // NH
W = J * 128
ROWS = XR * CZ
LOGJ = J.bit_length() - 1
BR = 32
F32 = jnp.float32
BF16 = jnp.bfloat16


def split(a):
    hi = a.astype(BF16)
    return hi, (a - hi.astype(F32)).astype(BF16)


def dot(a, b):
    return jnp.dot(a, b, preferred_element_type=F32)


def dot3(a, b):
    return dot(a[0], b[0]) + (dot(a[0], b[1]) + dot(a[1], b[0]))


def lanes(shape):
    return lax.broadcasted_iota(jnp.int32, shape, 1)


def roll(a, shift):
    return pltpu.roll(a, shift % 128, 1)


def exchange_lanes(tiles):
    tiles = list(tiles)
    group = lanes((8, 128)) // KL
    step = 1
    while step < XL:
        clear = (group & step) == 0
        for i in range(XL):
            if not i & step:
                k = i | step
                a, b = tiles[i], tiles[k]
                tiles[i] = jnp.where(clear, a, roll(b, step * KL))
                tiles[k] = jnp.where(clear, roll(a, -step * KL), b)
        step *= 2
    return tiles


def main_kernel(
    e_h, n_h, w_h, o_h, hh_h, hl_h, sh_h, sl_h, lam_h, mu_h, mup_h,
    p_v, f_v, src_v, zp_v, zf_v, e_v, n_v, w_v,
    o_v, hh, hl, sh, sl, lam, mu, mup,
    wa_v, zs_v, zps_v, y_v, send1, recv1, dh, dl, x_v, ea_v, eb_v, r_v, c_v, ag_v, uv_v, send2, recv2, zz_v,
    load_sem, halo_s, halo_r, a_s, a_r, g_s, g_r, b_s, b_r, ph_s, ph_r,
):
    me = lax.axis_index("gz")
    xi = lax.axis_index("xy")

    def gz(o):
        return {"gz": lax.rem(me + o, GZ)}

    def xy(o):
        return {"xy": lax.rem(xi + o, XY)}

    def load(k, src, dst):
        copy = pltpu.make_async_copy(src, dst, load_sem.at[k])
        copy.start()
        return copy

    def remote(src, dst, ssem, rsem, who):
        copy = pltpu.make_async_remote_copy(
            src_ref=src, dst_ref=dst, send_sem=ssem, recv_sem=rsem, device_id=who,
            device_id_type=pl.DeviceIdType.MESH,
        )
        copy.start()
        return copy

    loads = [
        load(0, o_h, o_v),
        load(1, w_h, w_v),
        load(2, e_h, e_v.at[pl.ds(0, ROWS)]),
        load(3, n_h, n_v),
        load(4, hh_h, hh),
        load(5, hl_h, hl),
        load(6, sh_h, sh),
        load(7, sl_h, sl),
        load(8, lam_h, lam),
        load(9, mu_h, mu),
        load(10, mup_h, mup),
    ]

    barrier = pltpu.get_barrier_semaphore()

    def greet_gz(o, _):
        pl.semaphore_signal(barrier, inc=1, device_id=gz(o), device_id_type=pl.DeviceIdType.MESH)
        return 0

    def greet_xy(o, _):
        pl.semaphore_signal(barrier, inc=1, device_id=xy(o), device_id_type=pl.DeviceIdType.MESH)
        return 0

    lax.fori_loop(1, GZ, greet_gz, 0)
    lax.fori_loop(1, XY, greet_xy, 0)

    with jax.named_scope("fluid"):
        loads[0].wait()

        def to_fluid(i, _):
            rows = pl.ds(pl.multiple_of(i * 64, 64), 64)
            f_v[pl.ds(pl.multiple_of(8 + i * 64, 8), 64), :] = (1 - o_v[rows, :]).astype(F32)
            return 0

        lax.fori_loop(0, ROWS // 64, to_fluid, 0)
        loads[1].wait()
        loads[2].wait()

        def edge(i, _):
            for k in range(8):
                x = i * 8 + k
                zs_v[pl.ds(x, 1), :] = f_v[pl.ds(x * 8 + 15, 1), :]
                zs_v[pl.ds(XR + x, 1), :] = f_v[pl.ds(x * 8 + 8, 1), :]
                zs_v[pl.ds(2 * XR + x, 1), :] = w_v[pl.ds(x * 8, 1), :]
            return 0

        lax.fori_loop(0, XR // 8, edge, 0)
    with jax.named_scope("barrier"):
        pl.semaphore_wait(barrier, GZ - 1 + XY - 1)
    halos = [
        remote(zs_v.at[pl.ds(2 * XR, XR)], wa_v, halo_s.at[0], halo_r.at[0], gz(GZ - 1)),
        remote(zs_v.at[pl.ds(XR, XR)], zf_v.at[pl.ds(XR, XR)], halo_s.at[1], halo_r.at[1], gz(GZ - 1)),
        remote(zs_v.at[pl.ds(0, XR)], zf_v.at[pl.ds(0, XR)], halo_s.at[2], halo_r.at[2], gz(1)),
        remote(f_v.at[pl.ds(ROWS, 8)], f_v.at[pl.ds(0, 8)], halo_s.at[3], halo_r.at[3], xy(1)),
        remote(f_v.at[pl.ds(8, 8)], f_v.at[pl.ds(ROWS + 8, 8)], halo_s.at[4], halo_r.at[4], xy(XY - 1)),
        remote(e_v.at[pl.ds(0, 8)], e_v.at[pl.ds(ROWS, 8)], halo_s.at[5], halo_r.at[5], xy(XY - 1)),
    ]
    with jax.named_scope("waithalo"):
        loads[3].wait()
        for k in range(4, 11):
            loads[k].wait()
        for h in halos:
            h.wait()

    sub = lax.broadcasted_iota(jnp.int32, (8, NY), 0)
    first = me == 0
    last = me == GZ - 1

    with jax.named_scope("source"):
        def source(i, _):
            base = pl.multiple_of(i * 8, 8)
            here = pl.ds(base, 8)
            f = f_v[pl.ds(pl.multiple_of(base + 8, 8), 8), :]
            fw = f_v[here, :]
            fe = f_v[pl.ds(pl.multiple_of(base + 16, 8), 8), :]
            east = f * (fw * e_v[here, :] - fe * e_v[pl.ds(pl.multiple_of(base + 8, 8), 8), :])
            fn = f * pltpu.roll(f, 1, 1) * n_v[here, :]
            north = fn - pltpu.roll(fn, NY - 1, 1)
            w = w_v[here, :]
            below = jnp.broadcast_to(zf_v[pl.ds(i, 1), :], (8, NY))
            above = jnp.broadcast_to(zf_v[pl.ds(XR + i, 1), :], (8, NY))
            wabove = jnp.broadcast_to(wa_v[pl.ds(i, 1), :], (8, NY))
            below = jnp.where(first, 1.0, below)
            above = jnp.where(last, 0.0, above)
            fb = jnp.where(sub == 0, below, pltpu.roll(f, 1, 0))
            fa = jnp.where(sub == 7, above, pltpu.roll(f, 7, 0))
            wn = jnp.where(sub == 7, wabove, pltpu.roll(w, 7, 0))
            up = f * (fb * w - fa * wn)
            src_v[here, :] = east + north + up
            return 0

        lax.fori_loop(0, XR, source, 0, unroll=4)

    def wait_bytes(ref, sem):
        pltpu.make_async_copy(ref, ref, sem).wait()

    for h in range(NH):
        hcol = pl.ds(h * LH, LH)

        with jax.named_scope("forward"):
            def forward(i, _):
                rows = pl.ds(pl.multiple_of(i * 256, 256), 256)
                y_v[rows, :] = dot3(split(src_v[rows, :]), (hh[:, hcol], hl[:, hcol]))
                return 0

            lax.fori_loop(0, ROWS // 256, forward, 0)

        with jax.named_scope("pack"):
            def pack(j, _):
                for t in range(LH // 128):
                    tiles = exchange_lanes(
                        [y_v[pl.ds(pl.multiple_of((x * J + j) * 8, 8), 8), pl.ds(t * 128, 128)] for x in range(XL)]
                    )
                    for a in range(XL):
                        send1[pl.ds((h * GZ + t * XL + a) * 8, 8), pl.ds(pl.multiple_of(j * 128, 128), 128)] = tiles[a]
                return 0

            lax.fori_loop(0, J, pack, 0)

        with jax.named_scope("send"):
            mine = pl.ds(pl.multiple_of(h * NZ + me * 8, 8), 8)

            def go(o, _):
                to = lax.rem(me + o, GZ)
                remote(
                    send1.at[pl.ds(pl.multiple_of((h * GZ + to) * 8, 8), 8)], recv1.at[mine],
                    a_s.at[h], a_r.at[h], {"gz": to},
                )
                return 0

            lax.fori_loop(1, GZ, go, 0)
            recv1[mine, :] = send1[pl.ds(pl.multiple_of((h * GZ + me) * 8, 8), 8), :]

    for h in range(NH):
        with jax.named_scope("rates"):
            lrow = lam[pl.ds(h * GZ + me, 1), :]

            def rates(i, _):
                rows = pl.ds(pl.multiple_of(i * 16, 16), 16)
                out = pl.ds(pl.multiple_of(h * NZ + i * 16, 16), 16)
                g = mu[rows, :] + lrow
                root = jnp.sqrt(g + 0.25 * g * g)
                r_v[out, :] = 1.0 / (1.0 + 0.5 * g + root)
                c_v[out, :] = (1.0 / (NZ + 1) / NY) / root
                return 0

            lax.fori_loop(0, NZ // 16, rates, 0)

    group = lanes((16, 128)) // KL
    wide = lanes((BR, 128)) // KL
    home = (lax.broadcasted_iota(jnp.int32, (BR, 128), 0) // 16) - wide

    for h in range(NH):
        with jax.named_scope("waita2a"):
            wait_bytes(recv1.at[pl.ds(h * NZ, NZ - 8)], a_r.at[h])

        with jax.named_scope("dst"):
            def cut(i, _):
                rows = pl.ds(pl.multiple_of(i * 16, 16), 16)
                a, b = split(recv1[pl.ds(pl.multiple_of(h * NZ + i * 16, 16), 16), :])
                dh[rows, :] = a
                dl[rows, :] = b
                return 0

            lax.fori_loop(0, NZ // 16, cut, 0)
            for c in range(W // 256):
                col = pl.ds(c * 256, 256)
                x_v[pl.ds(h * NZ, NZ), col] = dot3((sh[...], sl[...]), (dh[:, col], dl[:, col]))

        with jax.named_scope("sums"):
            def sums(i, carry):
                pa, pb = carry
                rows = pl.ds(pl.multiple_of(h * NZ + i * BR, BR), BR)
                r = r_v[rows, :]
                s = [x_v[rows, pl.ds(j * 128, 128)] for j in range(J)]
                u = [s[0]]
                for j in range(1, J):
                    u.append(s[j] + r * u[-1])
                v = [s[-1]]
                for j in range(J - 2, -1, -1):
                    v.append(s[j] + r * v[-1])
                v = v[::-1]
                for j in range(J):
                    x_v[rows, pl.ds(j * 128, 128)] = u[j] + v[j] - s[j]
                a, b = u[-1], v[0]
                pw = r
                for _ in range(LOGJ):
                    pw = pw * pw
                step = 1
                while step < XL:
                    a = a + jnp.where(wide >= step, pw * roll(a, step * KL), 0.0)
                    b = b + jnp.where(wide < XL - step, pw * roll(b, -step * KL), 0.0)
                    pw = pw * pw
                    step *= 2
                ea_v[rows, :] = jnp.where(wide >= 1, roll(a, KL), 0.0)
                eb_v[rows, :] = jnp.where(wide < XL - 1, roll(b, -KL), 0.0)
                for k in range(BR // 16):
                    q = i * (BR // 16) + k
                    at = group == q
                    cut16 = slice(k * 16, k * 16 + 16)
                    pa = jnp.where(at, pltpu.roll(a[cut16], lax.rem((q + 1) * KL, 128), 1), pa)
                    pb = jnp.where(at, pltpu.roll(b[cut16], q * KL, 1), pb)
                return pa, pb

            zero = jnp.zeros((16, 128), F32)
            pa, pb = lax.fori_loop(0, NZ // BR, sums, (zero, zero))
        with jax.named_scope("gather"):
            own = pl.ds(pl.multiple_of((h * XY + xi) * 32, 32), 32)
            ag_v[pl.ds(pl.multiple_of((h * XY + xi) * 32, 32), 16), :] = pa
            ag_v[pl.ds(pl.multiple_of((h * XY + xi) * 32 + 16, 16), 16), :] = pb

            def spread(o, _):
                remote(ag_v.at[own], ag_v.at[own], g_s.at[h], g_r.at[h], xy(o))
                return 0

            lax.fori_loop(1, XY, spread, 0)

    for h in range(NH):
        with jax.named_scope("waitgather"):
            wait_bytes(ag_v.at[pl.ds(h * XY * 32, (XY - 1) * 32)], g_r.at[h])
        with jax.named_scope("carry"):
            g = mup[...] + lam[pl.ds(h * GZ + me, 1), :]
            rp = 1.0 / (1.0 + 0.5 * g + jnp.sqrt(g + 0.25 * g * g))
            for _ in range(XR.bit_length() - 1):
                rp = rp * rp
            full = rp
            for _ in range(XY.bit_length() - 1):
                full = full * full
            close = 1.0 / (1.0 - full)

            def piece(o, part):
                at = (h * XY + lax.rem(xi + o, XY)) * 32 + part * 16
                return ag_v[pl.ds(pl.multiple_of(at, 16), 16), :]

            un, vn = piece(0, 0), piece(0, 1)
            for o in range(1, XY):
                un = un * rp + piece(o, 0)
                vn = vn * rp + piece(XY - o, 1)
            un = un * close
            vn = vn * close

        with jax.named_scope("finish"):
            def finish(i, _):
                rows = pl.ds(pl.multiple_of(h * NZ + i * BR, BR), BR)
                out = pl.ds(pl.multiple_of(i * BR, BR), BR)
                at = home == -(i * (BR // 16))
                ub = jnp.where(at, jnp.concatenate([un] * (BR // 16), 0), 0.0)
                vb = jnp.where(at, jnp.concatenate([vn] * (BR // 16), 0), 0.0)
                step = 1
                while step < XL:
                    ub = ub + roll(ub, step * KL)
                    vb = vb + roll(vb, step * KL)
                    step *= 2
                r = r_v[rows, :]
                powers = [r]
                for _ in range(J - 1):
                    powers.append(powers[-1] * r)
                pw = powers[-1]
                up = jnp.ones_like(r)
                down = jnp.ones_like(r)
                step = 1
                while step < XL:
                    on = (wide & step) != 0
                    up = jnp.where(on, up * pw, up)
                    down = jnp.where(on, down, down * pw)
                    pw = pw * pw
                    step *= 2
                cu = ea_v[rows, :] + up * ub
                cv = eb_v[rows, :] + down * vb
                c = c_v[rows, :]
                for j in range(J):
                    col = pl.ds(j * 128, 128)
                    sol = c * (x_v[rows, col] + powers[j] * cu + powers[J - 1 - j] * cv)
                    a, b = split(sol)
                    dh[out, col] = a
                    dl[out, col] = b
                return 0

            lax.fori_loop(0, NZ // BR, finish, 0)
        with jax.named_scope("idst"):
            for c in range(W // 256):
                col = pl.ds(c * 256, 256)
                send2[pl.ds(h * NZ, NZ), col] = dot3((sh[...], sl[...]), (dh[:, col], dl[:, col]))

        with jax.named_scope("back"):
            mine = pl.ds(pl.multiple_of((h * GZ + me) * 8, 8), 8)

            def back(o, _):
                to = lax.rem(me + o, GZ)
                remote(
                    send2.at[pl.ds(pl.multiple_of(h * NZ + to * 8, 8), 8)], recv2.at[mine],
                    b_s.at[h], b_r.at[h], {"gz": to},
                )
                return 0

            lax.fori_loop(1, GZ, back, 0)
            recv2[mine, :] = send2[pl.ds(pl.multiple_of(h * NZ + me * 8, 8), 8), :]

    for h in range(NH):
        with jax.named_scope("waitback"):
            wait_bytes(recv2.at[pl.ds(h * NZ, NZ - 8)], b_r.at[h])

        with jax.named_scope("unpack"):
            def unpack(j, _):
                for t in range(LH // 128):
                    tiles = exchange_lanes(
                        [
                            recv2[pl.ds((h * GZ + t * XL + a) * 8, 8), pl.ds(pl.multiple_of(j * 128, 128), 128)]
                            for a in range(XL)
                        ]
                    )
                    for x in range(XL):
                        zz_v[pl.ds(pl.multiple_of((x * J + j) * 8, 8), 8), pl.ds(t * 128, 128)] = tiles[x]
                return 0

            lax.fori_loop(0, J, unpack, 0)

        with jax.named_scope("inverse"):
            def inverse(i, _):
                rows = pl.ds(pl.multiple_of(i * 256, 256), 256)
                out = pl.ds(pl.multiple_of(8 + i * 256, 8), 256)
                hrow = pl.ds(h * LH, LH)
                part = dot3(split(zz_v[rows, :]), (hh[hrow, :], hl[hrow, :]))
                p_v[out, :] = part if h == 0 else p_v[out, :] + part
                return 0

            lax.fori_loop(0, ROWS // 256, inverse, 0)

    with jax.named_scope("pplanes"):
        def pedge(i, _):
            for k in range(8):
                x = i * 8 + k
                zps_v[pl.ds(x, 1), :] = p_v[pl.ds(x * 8 + 15, 1), :]
                zps_v[pl.ds(XR + x, 1), :] = p_v[pl.ds(x * 8 + 8, 1), :]
            return 0

        lax.fori_loop(0, XR // 8, pedge, 0)
        planes = [
            remote(zps_v.at[pl.ds(0, XR)], zp_v.at[pl.ds(0, XR)], ph_s.at[0], ph_r.at[0], gz(1)),
            remote(zps_v.at[pl.ds(XR, XR)], zp_v.at[pl.ds(XR, XR)], ph_s.at[1], ph_r.at[1], gz(GZ - 1)),
            remote(p_v.at[pl.ds(ROWS, 8)], p_v.at[pl.ds(0, 8)], ph_s.at[2], ph_r.at[2], xy(1)),
            remote(p_v.at[pl.ds(8, 8)], p_v.at[pl.ds(ROWS + 8, 8)], ph_s.at[3], ph_r.at[3], xy(XY - 1)),
        ]
    with jax.named_scope("waitend"):
        for h in range(NH):
            wait_bytes(send1.at[pl.ds(h * NZ, NZ - 8)], a_s.at[h])
            wait_bytes(ag_v.at[pl.ds(h * XY * 32, (XY - 1) * 32)], g_s.at[h])
            wait_bytes(send2.at[pl.ds(h * NZ, NZ - 8)], b_s.at[h])
        for c in planes:
            c.wait()


def last_kernel(e, n, w, src, p_v, f_v, zp, zf, eo, no, wo, po, ro):
    step = pl.program_id(0)
    me = lax.axis_index("gz")
    first = me == 0
    last = me == GZ - 1
    sub = lax.broadcasted_iota(jnp.int32, (8, NY), 0)

    def one(i, _):
        here = pl.ds(pl.multiple_of(i * 8, 8), 8)
        x = step * 8 + i
        base = pl.multiple_of(x * 8, 8)
        mid = pl.ds(pl.multiple_of(base + 8, 8), 8)
        east = pl.ds(pl.multiple_of(base + 16, 8), 8)
        p = p_v[mid, :]
        f = f_v[mid, :]
        below = jnp.where(first, 1.0, jnp.broadcast_to(zf[pl.ds(x, 1), :], (8, NY)))
        above = jnp.where(last, 0.0, jnp.broadcast_to(zf[pl.ds(XR + x, 1), :], (8, NY)))
        pbelow = jnp.where(first, 0.0, jnp.broadcast_to(zp[pl.ds(x, 1), :], (8, NY)))
        pabove = jnp.broadcast_to(zp[pl.ds(XR + x, 1), :], (8, NY))
        oe = f * f_v[pl.ds(base, 8), :]
        oe_next = f * f_v[east, :]
        on = f * pltpu.roll(f, 1, 1)
        on_next = pltpu.roll(on, NY - 1, 1)
        ou = f * jnp.where(sub == 0, below, pltpu.roll(f, 1, 0))
        ou_next = f * jnp.where(sub == 7, above, pltpu.roll(f, 7, 0))
        de = p - p_v[pl.ds(base, 8), :]
        de_next = p - p_v[east, :]
        dn = p - pltpu.roll(p, 1, 1)
        dn_next = p - pltpu.roll(p, NY - 1, 1)
        du = p - jnp.where(sub == 0, pbelow, pltpu.roll(p, 1, 0))
        du_next = p - jnp.where(sub == 7, pabove, pltpu.roll(p, 7, 0))
        applied = oe * de + oe_next * de_next + on * dn + on_next * dn_next + ou * du + ou_next * du_next
        ro[here, :] = src[here, :] - applied
        eo[here, :] = oe * (e[here, :] - de)
        no[here, :] = on * (n[here, :] - dn)
        wo[here, :] = ou * (w[here, :] - du)
        po[here, :] = p
        return 0

    lax.fori_loop(0, 8, one, 0, unroll=4)


def tables():
    i = np.arange(NY)
    angle = 2 * np.pi * ((i[:, None] * i[None, :]) % NY) / NY
    hart = np.cos(angle) + np.sin(angle)
    k = np.arange(1, NZ + 1)
    sine = np.sin(np.pi * ((k[:, None] * k[None, :]) % (2 * (NZ + 1))) / (NZ + 1))
    lam = 4 * np.sin(np.pi * i / NY) ** 2
    mu = 4 * np.sin(np.pi * k / (2 * (NZ + 1))) ** 2

    def cut(a):
        hi = a.astype(np.float32).astype(BF16)
        return hi, (a - hi.astype(np.float64)).astype(np.float32).astype(BF16)

    lanes_of = np.arange(128)
    half = np.arange(NH)[:, None, None]
    who = np.arange(GZ)[None, :, None]
    lam = lam[half * LH + who * KL + lanes_of[None, None, :] % KL].reshape(NH * GZ, 128)
    packed = mu[(lanes_of[None, :] // KL) * 16 + np.arange(16)[:, None]]
    mu = np.repeat(mu[:, None], 128, 1)
    return (*cut(hart), *cut(sine), lam.astype(np.float32), mu.astype(np.float32), packed.astype(np.float32))


def local(east_velocity, north_velocity, upward_velocity, obstacle):
    fields = (east_velocity, north_velocity, upward_velocity, obstacle)
    args = [pltpu.with_memory_space_constraint(a.reshape(ROWS, NY), pltpu.HBM) for a in fields]
    args += [pltpu.with_memory_space_constraint(jnp.asarray(t), pltpu.HBM) for t in tables()]
    any_spec = pl.BlockSpec(memory_space=pl.ANY)
    vmem = pl.BlockSpec(memory_space=pltpu.VMEM)
    ext = jax.ShapeDtypeStruct((ROWS + 16, NY), F32)
    planes = jax.ShapeDtypeStruct((2 * XR, NY), F32)

    def v(*shape, dtype=F32):
        return pltpu.VMEM(shape, dtype)

    dma = pltpu.SemaphoreType.DMA
    field = jax.ShapeDtypeStruct((ROWS, NY), F32)
    longer = jax.ShapeDtypeStruct((ROWS + 8, NY), F32)
    p, f, src, zp, zf, e, n, w = pl.pallas_call(
        main_kernel,
        out_shape=[ext, ext, field, planes, planes, longer, field, field],
        in_specs=[any_spec] * 11,
        out_specs=[vmem] * 8,
        scratch_shapes=[
            v(ROWS, NY, dtype=jnp.int32),
            v(NY, NY, dtype=BF16), v(NY, NY, dtype=BF16), v(NZ, NZ, dtype=BF16), v(NZ, NZ, dtype=BF16),
            v(NH * GZ, 128), v(NZ, 128), v(16, 128),
            v(XR, NY), v(3 * XR, NY), v(2 * XR, NY),
            v(ROWS, LH), v(NH * NZ, W), v(NH * NZ, W), v(NZ, W, dtype=BF16), v(NZ, W, dtype=BF16),
            v(NH * NZ, W), v(NH * NZ, 128), v(NH * NZ, 128), v(NH * NZ, 128), v(NH * NZ, 128),
            v(NH * XY * 32, 128), v(32, 128), v(NH * NZ, W), v(NH * NZ, W), v(ROWS, LH),
            dma((11,)), dma((6,)), dma((6,)), dma((NH,)), dma((NH,)), dma((NH,)), dma((NH,)),
            dma((NH,)), dma((NH,)), dma((4,)), dma((4,)),
        ],
        compiler_params=pltpu.CompilerParams(
            collective_id=0, has_side_effects=True, vmem_limit_bytes=32 * 1024 * 1024
        ),
        name="main",
    )(*args)

    block = pl.BlockSpec((64, NY), lambda i: (i, 0))
    outs = pl.pallas_call(
        last_kernel,
        grid=(ROWS // 64,),
        out_shape=[field] * 5,
        in_specs=[block] * 4 + [pl.BlockSpec(a.shape, lambda i: (0, 0)) for a in (p, f, zp, zf)],
        out_specs=[block] * 5,
        compiler_params=pltpu.CompilerParams(vmem_limit_bytes=16 * 1024 * 1024),
        name="last",
    )(e, n, w, src, p, f, zp, zf)
    return tuple(a.reshape(XR, CZ, NY) for a in outs)


def solution(mesh):
    spec = P("xy", "gz", None)
    return jax.shard_map(local, mesh=mesh, in_specs=(spec,) * 4, out_specs=(spec,) * 5, check_vma=False)
```

time: 103 us -> 71.8 us (0.70)
  Pallas kernels: 90.4 us -> 71.1 us
  local copies, waits for them, and re-layouts: 11.1 us -> 0 us
    pallas_call x2, Pallas kernels: 90.4 us -> 71.1 us  [the longest x1 66 us: local(): pl.pallas_call(main_kernel, out_shape=[ext, ext, field, planes, planes, l...]
    unnamed x22 -> x0, local copies, waits for them, and re-layouts: 11.1 us -> none
where the time goes in v2:
time: 71.8 us; the launch traced here: 71.7 us
  Pallas kernels  71.1 us (99%)
    pallas_call x1, Pallas kernels, local(): pl.pallas_call(main_kernel, out_shape=[ext, ext, field, planes, planes, l...  66 us
    pallas_call x1, Pallas kernels, local(): pl.pallas_call(last_kernel, grid=(ROWS // 64,), out_shape=[field] * 5, in...  5.07 us

profile of v2, /device:TPU:2, one launch (start us, length us, event | category | flops | bytes accessed | tf_op | source)
XLA Modules:
  0.0 71.7 jit_solution(14067795854063531415)
XLA Ops:
  0.6 66.0 %main.1 = (f32[528,512]{1,0:T(8,128)S(1)}, f32[528,512]{1,0:T(8,128)S(1)}, f32[512,512]{1,0:T(8,128)S(1)}, f32[128,512]{1,0:T(8,128)S(1)}, f32[128,512]{1,0:T(8,...) custom-call(f32[512,512]{1,0:T(8,128)} %bitcast.9, f32[512,512]{1,0:T(8,128)} %bitcast.10, ...), custom_call_target="tpu_custom_call" | custom-call | tf_op jit(solution)/shard_map/main/pallas_call | solution.py:529
  66.6 5.1 %last.1 = (f32[512,512]{1,0:T(8,128)}, f32[512,512]{1,0:T(8,128)}, f32[512,512]{1,0:T(8,128)}, f32[512,512]{1,0:T(8,128)}, f32[512,512]{1,0:T(8,128)}) custom-call(f32[520,512]{1,0:T(8,128)S(1)} %get-tuple-element.18.e, f32[512,512]{1,0:T(8,128)S(1)} %get-tuple-element.19.n, f32[512,512]{1,0:T(8,128)S(1)} %get-tuple-element.20.w, ...), custom_call_target="tpu_custom_call" | custom-call | tf_op jit(solution)/shard_map/last/pallas_call | solution.py:552

commit v3 on v2

v3 whole, which is shorter than its diff:
```python
import functools

import jax
import jax.numpy as jnp
import numpy as np
from jax import lax
from jax.experimental import pallas as pl
from jax.experimental.pallas import tpu as pltpu
from jax.sharding import PartitionSpec as P

NX = 512
NY = 512
NZ = 256
GZ = 32
XY = 8
XR = NX // XY
CZ = NZ // GZ
NH = 4
KL = NY // GZ // NH
XL = 128 // KL
J = XR // XL
LH = NY // NH
W = J * 128
ROWS = XR * CZ
LOGJ = J.bit_length() - 1
BR = 32
BW = 128
NG = LH // 128
PR = NZ // XL
LAG = 2
XS = 16
EDGE = 2 * XR + 16
F32 = jnp.float32
BF16 = jnp.bfloat16


def split(a):
    hi = a.astype(BF16)
    return hi, (a - hi.astype(F32)).astype(BF16)


def dot(a, b):
    return jnp.dot(a, b, preferred_element_type=F32)


def dot3(a, b):
    return dot(a[0], b[0]) + (dot(a[0], b[1]) + dot(a[1], b[0]))


def lanes(shape):
    return lax.broadcasted_iota(jnp.int32, shape, 1)


def slot(t):
    return t % NG * XL + t // NG


def far_first():
    hops = (0, 1, 2, 1)
    every = [(x, y, c) for x in range(4) for y in range(4) for c in range(2)]
    every.remove((0, 0, 0))
    return sorted(every, key=lambda o: -(hops[o[0]] + hops[o[1]]))


def roll(a, shift):
    return pltpu.roll(a, shift % 128, 1)


def exchange_lanes(tiles):
    tiles = list(tiles)
    group = lanes((8, 128)) // KL
    step = 1
    while step < XL:
        clear = (group & step) == 0
        for i in range(XL):
            if not i & step:
                k = i | step
                a, b = tiles[i], tiles[k]
                tiles[i] = jnp.where(clear, a, roll(b, step * KL))
                tiles[k] = jnp.where(clear, roll(a, -step * KL), b)
        step *= 2
    return tiles


def row(ref, r):
    return jnp.broadcast_to(ref[pl.ds(r, 1), :], (8, ref.shape[1]))


def tile8(at):
    return pl.ds(pl.multiple_of(at * 8, 8), 8)


def main_kernel(
    e_h, n_h, w_h, o_h, hh_h, hl_h, sh_h, sl_h, lam_h, mu_h, mup_h,
    p_v, eo_v, no_v, wo_v, ro_v, z0_v, z7_v,
    f_v, e_v, n_v, w_v, zp_v, zf_v, ga_v, px_v,
    o_v, src_v, hh, hl, sh, sl, lam, mu, mup,
    zs_v, gs_v, fx_v, ex_v, cc_v, cy_v, zb_v, pb_v, up_v, dn_v,
    y_v, send1, recv1, dh, dl, x_v, ea_v, eb_v, r_v, c_v, ag_v, send2, recv2, zz_v,
    load_sem, halo_s, halo_r, a_s, a_r, g_s, g_r, b_s, b_r, ph_s, ph_r,
):
    me = lax.axis_index("gz")
    xi = lax.axis_index("xy")
    first = me == 0
    last = me == GZ - 1
    spot = lax.rem(me, NG) * XL + me // NG

    def gz(o):
        return {"gz": lax.rem(me + o, GZ)}

    def xy(o):
        return {"xy": lax.rem(xi + o, XY)}

    def peer(o):
        x = lax.rem(me // 8 + o[0], 4)
        y = lax.rem(me // 2 + o[1], 4)
        return (x * 4 + y) * 2 + lax.rem(me + o[2], 2)

    def load(k, src, dst):
        copy = pltpu.make_async_copy(src, dst, load_sem.at[k])
        copy.start()
        return copy

    def remote(src, dst, ssem, rsem, who):
        copy = pltpu.make_async_remote_copy(
            src_ref=src, dst_ref=dst, send_sem=ssem, recv_sem=rsem, device_id=who,
            device_id_type=pl.DeviceIdType.MESH,
        )
        copy.start()
        return copy

    def wait_bytes(ref, sem):
        pltpu.make_async_copy(ref, ref, sem).wait()

    flags = load(0, o_h, o_v)
    barrier = pltpu.get_barrier_semaphore()

    def greet_gz(o, _):
        pl.semaphore_signal(barrier, inc=1, device_id=gz(o), device_id_type=pl.DeviceIdType.MESH)
        return 0

    def greet_xy(o, _):
        pl.semaphore_signal(barrier, inc=1, device_id=xy(o), device_id_type=pl.DeviceIdType.MESH)
        return 0

    lax.fori_loop(1, GZ, greet_gz, 0)
    lax.fori_loop(1, XY, greet_xy, 0)

    loads = [
        flags,
        load(1, w_h, w_v),
        load(2, e_h, e_v.at[pl.ds(0, ROWS)]),
        load(3, n_h, n_v),
        load(4, hh_h, hh),
        load(5, hl_h, hl),
        load(6, sh_h, sh),
        load(7, sl_h, sl),
        load(8, lam_h, lam),
        load(9, mu_h, mu),
        load(10, mup_h, mup),
    ]

    with jax.named_scope("fluid"):
        loads[0].wait()

        def to_fluid(i, _):
            rows = pl.ds(pl.multiple_of(i * 64, 64), 64)
            f_v[pl.ds(pl.multiple_of(8 + i * 64, 8), 64), :] = (1 - o_v[rows, :]).astype(F32)
            return 0

        lax.fori_loop(0, ROWS // 64, to_fluid, 0)
        f_v[pl.ds(0, 8), :] = jnp.zeros((8, NY), F32)
        f_v[pl.ds(ROWS + 8, 8), :] = jnp.zeros((8, NY), F32)
        e_v[pl.ds(ROWS, 8), :] = jnp.zeros((8, NY), F32)
        loads[1].wait()

        def edge(i, _):
            for k in range(8):
                x = i * 8 + k
                low = f_v[pl.ds(x * 8 + 8, 1), :]
                zs_v[pl.ds(x, 1), :] = f_v[pl.ds(x * 8 + 15, 1), :]
                zs_v[pl.ds(XR + x, 1), :] = low
                gs_v[pl.ds(x, 1), :] = low * w_v[pl.ds(x * 8, 1), :]
            return 0

        lax.fori_loop(0, XR // 8, edge, 0)
        loads[2].wait()
    with jax.named_scope("barrier"):
        pl.semaphore_wait(barrier, GZ - 1 + XY - 1)
    halos = [
        remote(gs_v, ga_v, halo_s.at[0], halo_r.at[0], gz(GZ - 1)),
        remote(zs_v.at[pl.ds(0, XR)], zf_v.at[pl.ds(0, XR)], halo_s.at[1], halo_r.at[1], gz(1)),
        remote(f_v.at[pl.ds(ROWS, 8)], fx_v.at[pl.ds(0, 8)], halo_s.at[2], halo_r.at[2], xy(1)),
        remote(f_v.at[pl.ds(8, 8)], fx_v.at[pl.ds(8, 8)], halo_s.at[3], halo_r.at[3], xy(XY - 1)),
        remote(e_v.at[pl.ds(0, 8)], ex_v, halo_s.at[4], halo_r.at[4], xy(XY - 1)),
        remote(zs_v.at[pl.ds(XR, XR)], zf_v.at[pl.ds(XR, XR)], halo_s.at[5], halo_r.at[5], gz(GZ - 1)),
    ]

    with jax.named_scope("source"):
        loads[3].wait()
        sub = lax.broadcasted_iota(jnp.int32, (8, NY), 0)

        def source(i, _):
            def east(x):
                return f_v[tile8(x + 1), :] * f_v[tile8(x), :] * e_v[tile8(x), :]

            now = east(i * 8)
            for k in range(8):
                x = i * 8 + k
                then = east(x + 1)
                f = f_v[tile8(x + 1), :]
                north = f * pltpu.roll(f, 1, 1) * n_v[tile8(x), :]
                up = jnp.where(sub == 0, 0.0, f * pltpu.roll(f, 1, 0) * w_v[tile8(x), :])
                src_v[tile8(x), :] = (now - then) + (north - pltpu.roll(north, NY - 1, 1)) + (up - pltpu.roll(up, 7, 0))
                now = then
            return 0

        lax.fori_loop(0, XR // 8, source, 0)

    with jax.named_scope("forward"):
        for k in range(4, 11):
            loads[k].wait()

        def forward(i, _):
            y = dot3(split(src_v[pl.ds(pl.multiple_of(i * 128, 128), 128), :]), (hh[...], hl[...]))
            for h in range(NH):
                out = pl.ds(pl.multiple_of(h * ROWS + i * 128, 128), 128)
                y_v[out, :] = y[:, h * LH : h * LH + LH]
            return 0

        lax.fori_loop(0, ROWS // 128, forward, 0)

    with jax.named_scope("waithalo"):
        for h in halos[:5]:
            h.wait()

    with jax.named_scope("edges"):
        low, high = pl.ds(0, XR), pl.ds(XR, XR)
        cc_v[low, :] = jnp.where(first, 1.0, zf_v[low, :]) * gs_v[...]
        cc_v[high, :] = jnp.where(last, 0.0, zs_v[low, :] * ga_v[...] * -1.0)
        cc_v[pl.ds(2 * XR, 8), :] = fx_v[pl.ds(0, 8), :] * f_v[pl.ds(8, 8), :] * e_v[pl.ds(0, 8), :]
        cc_v[pl.ds(2 * XR + 8, 8), :] = f_v[pl.ds(ROWS, 8), :] * fx_v[pl.ds(8, 8), :] * ex_v[...] * -1.0
        cy = dot3(split(cc_v[...]), (hh[...], hl[...]))
        for h in range(NH):
            part = cy[:, h * LH : h * LH + LH]
            cy_v[h] = part
            lo, hi = pl.ds(h * ROWS, 8), pl.ds(h * ROWS + ROWS - 8, 8)
            y_v[lo, :] = y_v[lo, :] + part[2 * XR : 2 * XR + 8]
            y_v[hi, :] = y_v[hi, :] + part[2 * XR + 8 :]

    sub1 = lax.broadcasted_iota(jnp.int32, (8, 128), 0)
    for h in range(NH):
        with jax.named_scope("pack"):
            mine = pl.ds(pl.multiple_of(h * NZ + me * 8, 8), 8)
            for t in range(NG):
                tcol = pl.ds(t * 128, 128)

                for j in range(J):
                    tiles = []
                    for a in range(XL):
                        x = a * J + j
                        below = jnp.broadcast_to(cy_v[h, pl.ds(x, 1), tcol], (8, 128))
                        above = jnp.broadcast_to(cy_v[h, pl.ds(XR + x, 1), tcol], (8, 128))
                        extra = jnp.where(sub1 == 0, below, jnp.where(sub1 == 7, above, 0.0))
                        tiles.append(y_v[pl.ds((h * XR + x) * 8, 8), tcol] + extra)
                    tiles = exchange_lanes(tiles)
                    for a in range(XL):
                        send1[pl.ds((h * GZ + t * XL + a) * 8, 8), pl.ds(j * 128, 128)] = tiles[a]

            for o in far_first():
                to = peer(o)
                place = lax.rem(to, NG) * XL + to // NG
                remote(send1.at[tile8(h * GZ + place)], recv1.at[mine], a_s.at[h], a_r.at[h], {"gz": to})
            recv1[mine, :] = send1[tile8(h * GZ + spot), :]

    with jax.named_scope("rates"):
        group_r = lanes((64, 128)) // KL
        for h in range(NH):
            lrow = lam[pl.ds(h * GZ + me, 1), :]

            def rates(i, _):
                rows = pl.ds(pl.multiple_of(i * 64, 64), 64)
                out = pl.ds(pl.multiple_of(h * NZ + i * 64, 64), 64)
                g = mu[rows, :] + lrow
                root = jnp.sqrt(g + 0.25 * g * g)
                r = 1.0 / (1.0 + 0.5 * g + root)
                r_v[out, :] = r
                c_v[out, :] = (1.0 / (NZ + 1) / NY) / root
                pw = r
                for _ in range(LOGJ):
                    pw = pw * pw
                up = jnp.ones_like(r)
                down = jnp.ones_like(r)
                step = 1
                while step < XL:
                    on = (group_r & step) != 0
                    up = jnp.where(on, up * pw, up)
                    down = jnp.where(on, down, down * pw)
                    pw = pw * pw
                    step *= 2
                up_v[out, :] = up
                dn_v[out, :] = down
                return 0

            lax.fori_loop(0, NZ // 64, rates, 0)

    group = lanes((PR, 128)) // KL
    wide = lanes((BW, 128)) // KL
    home = lax.broadcasted_iota(jnp.int32, (BW, 128), 0) // PR - wide
    QS = BW // PR

    def descend(h):
        with jax.named_scope("waita2a"):
            wait_bytes(recv1.at[pl.ds(h * NZ, NZ - 8)], a_r.at[h])

        with jax.named_scope("dst"):
            def cut(i, _):
                rows = pl.ds(pl.multiple_of(i * 32, 32), 32)
                a, b = split(recv1[pl.ds(pl.multiple_of(h * NZ + i * 32, 32), 32), :])
                dh[rows, :] = a
                dl[rows, :] = b
                return 0

            lax.fori_loop(0, NZ // 32, cut, 0)
            for c in range(W // 256):
                col = pl.ds(c * 256, 256)
                x_v[pl.ds(h * NZ, NZ), col] = dot3((sh[...], sl[...]), (dh[:, col], dl[:, col]))

        with jax.named_scope("sums"):
            def sums(i, _):
                rows = pl.ds(pl.multiple_of(h * NZ + i * BR, BR), BR)
                r = r_v[rows, :]
                s = [x_v[rows, pl.ds(j * 128, 128)] for j in range(J)]
                u = [s[0]]
                for j in range(1, J):
                    u.append(s[j] + r * u[-1])
                v = [s[-1]]
                for j in range(J - 2, -1, -1):
                    v.append(s[j] + r * v[-1])
                v = v[::-1]
                for j in range(J):
                    x_v[rows, pl.ds(j * 128, 128)] = u[j] + v[j] - s[j]
                ea_v[rows, :] = u[-1]
                eb_v[rows, :] = v[0]
                return 0

            lax.fori_loop(0, NZ // BR, sums, 0)
            pa = jnp.zeros((PR, 128), F32)
            pb = jnp.zeros((PR, 128), F32)
            for i in range(NZ // BW):
                rows = pl.ds(h * NZ + i * BW, BW)
                a, b = ea_v[rows, :], eb_v[rows, :]
                pw = r_v[rows, :]
                for _ in range(LOGJ):
                    pw = pw * pw
                step = 1
                while step < XL:
                    a = a + jnp.where(wide >= step, pw * roll(a, step * KL), 0.0)
                    b = b + jnp.where(wide < XL - step, pw * roll(b, -step * KL), 0.0)
                    pw = pw * pw
                    step *= 2
                ea_v[rows, :] = jnp.where(wide >= 1, roll(a, KL), 0.0)
                eb_v[rows, :] = jnp.where(wide < XL - 1, roll(b, -KL), 0.0)
                for k in range(QS):
                    q = i * QS + k
                    piece = slice(k * PR, k * PR + PR)
                    pa = jnp.where(group == q, roll(a[piece], (q + 1) * KL), pa)
                    pb = jnp.where(group == q, roll(b[piece], q * KL), pb)

        with jax.named_scope("gather"):
            at = pl.multiple_of((h * XY + xi) * 2 * PR, 2 * PR)
            own = pl.ds(at, 2 * PR)
            ag_v[pl.ds(at, PR), :] = pa
            ag_v[pl.ds(pl.multiple_of(at + PR, PR), PR), :] = pb

            def spread(o, _):
                remote(ag_v.at[own], ag_v.at[own], g_s.at[h], g_r.at[h], xy(o))
                return 0

            lax.fori_loop(1, XY, spread, 0)

    def ascend(h):
        with jax.named_scope("waitgather"):
            wait_bytes(ag_v.at[pl.ds(h * XY * 2 * PR, (XY - 1) * 2 * PR)], g_r.at[h])
        with jax.named_scope("finish"):
            g = mup[...] + lam[pl.ds(h * GZ + me, 1), :]
            rp = 1.0 / (1.0 + 0.5 * g + jnp.sqrt(g + 0.25 * g * g))
            for _ in range(XR.bit_length() - 1):
                rp = rp * rp
            full = rp
            for _ in range(XY.bit_length() - 1):
                full = full * full
            close = 1.0 / (1.0 - full)

            def piece(o, part):
                at = (h * XY + lax.rem(xi + o, XY)) * 2 * PR + part * PR
                return ag_v[pl.ds(pl.multiple_of(at, PR), PR), :]

            un, vn = piece(0, 0), piece(0, 1)
            for o in range(1, XY):
                un = un * rp + piece(o, 0)
                vn = vn * rp + piece(XY - o, 1)
            un = un * close
            vn = vn * close

            for i in range(NZ // BW):
                rows = pl.ds(h * NZ + i * BW, BW)
                at = home == -(i * QS)
                ub = jnp.where(at, jnp.concatenate([un] * QS, 0), 0.0)
                vb = jnp.where(at, jnp.concatenate([vn] * QS, 0), 0.0)
                step = 1
                while step < XL:
                    ub = ub + roll(ub, step * KL)
                    vb = vb + roll(vb, step * KL)
                    step *= 2
                ea_v[rows, :] = ea_v[rows, :] + up_v[rows, :] * ub
                eb_v[rows, :] = eb_v[rows, :] + dn_v[rows, :] * vb

            def finish(i, _):
                rows = pl.ds(pl.multiple_of(h * NZ + i * BR, BR), BR)
                out = pl.ds(pl.multiple_of(i * BR, BR), BR)
                r = r_v[rows, :]
                c = c_v[rows, :]
                cu = [r * ea_v[rows, :]]
                cv = [r * eb_v[rows, :]]
                for _ in range(J - 1):
                    cu.append(r * cu[-1])
                    cv.append(r * cv[-1])
                for j in range(J):
                    col = pl.ds(j * 128, 128)
                    a, b = split(c * (x_v[rows, col] + cu[j] + cv[J - 1 - j]))
                    dh[out, col] = a
                    dl[out, col] = b
                return 0

            lax.fori_loop(0, NZ // BR, finish, 0)

        with jax.named_scope("idst"):
            for c in range(W // 256):
                col = pl.ds(c * 256, 256)
                send2[pl.ds(h * NZ, NZ), col] = dot3((sh[...], sl[...]), (dh[:, col], dl[:, col]))

        with jax.named_scope("back"):
            mine = tile8(h * GZ + spot)

            for o in far_first():
                to = peer(o)
                remote(send2.at[tile8(h * GZ + to)], recv2.at[mine], b_s.at[h], b_r.at[h], {"gz": to})
            recv2[mine, :] = send2[tile8(h * GZ + me), :]

    for k in range(NH + LAG):
        if k < NH:
            descend(k)
        if k >= LAG:
            ascend(k - LAG)

    for h in range(NH):
        hrow = pl.ds(h * LH, LH)
        with jax.named_scope("waitback"):
            wait_bytes(recv2.at[pl.ds(h * NZ, NZ - 8)], b_r.at[h])

        with jax.named_scope("unpack"):
            for t in range(NG):
                for j in range(J):
                    tiles = exchange_lanes(
                        [recv2[pl.ds((h * GZ + t * XL + a) * 8, 8), pl.ds(j * 128, 128)] for a in range(XL)]
                    )
                    for a in range(XL):
                        zz_v[pl.ds((a * J + j) * 8, 8), pl.ds(t * 128, 128)] = tiles[a]

        with jax.named_scope("planes"):
            def border(i, _):
                for k in range(8):
                    x = i * 8 + k
                    zb_v[pl.ds(x, 1), :] = zz_v[pl.ds(x * 8, 1), :]
                    zb_v[pl.ds(XR + x, 1), :] = zz_v[pl.ds(x * 8 + 7, 1), :]
                return 0

            lax.fori_loop(0, XR // 8, border, 0)
            zb_v[pl.ds(2 * XR, 8), :] = zz_v[pl.ds(0, 8), :]
            zb_v[pl.ds(2 * XR + 8, 8), :] = zz_v[pl.ds(ROWS - 8, 8), :]
            part = dot3(split(zb_v[...]), (hh[hrow, :], hl[hrow, :]))
            pb_v[...] = part if h == 0 else pb_v[...] + part

        if h == NH - 1:
            planes = [
                remote(pb_v.at[pl.ds(XR, XR)], zp_v.at[pl.ds(0, XR)], ph_s.at[0], ph_r.at[0], gz(1)),
                remote(pb_v.at[pl.ds(0, XR)], zp_v.at[pl.ds(XR, XR)], ph_s.at[1], ph_r.at[1], gz(GZ - 1)),
                remote(pb_v.at[pl.ds(2 * XR + 8, 8)], px_v.at[pl.ds(0, 8)], ph_s.at[2], ph_r.at[2], xy(1)),
                remote(pb_v.at[pl.ds(2 * XR, 8)], px_v.at[pl.ds(8, 8)], ph_s.at[3], ph_r.at[3], xy(XY - 1)),
            ]

        with jax.named_scope("inverse"):
            def inverse(i, _):
                rows = pl.ds(pl.multiple_of(i * 256, 256), 256)
                out = rows
                part = dot3(split(zz_v[rows, :]), (hh[hrow, :], hl[hrow, :]))
                p_v[out, :] = part if h == 0 else p_v[out, :] + part
                return 0

            lax.fori_loop(0, ROWS // 256, inverse, 0)

    with jax.named_scope("outputs"):
        def outputs(i, _):
            def east(x, p, before):
                return f_v[tile8(x + 1), :] * f_v[tile8(x), :] * (e_v[tile8(x), :] - (p - before))

            p = p_v[tile8(i * 8), :]
            now = east(i * 8, p, p_v[tile8(jnp.maximum(i * 8 - 1, 0)), :])
            for k in range(8):
                x = i * 8 + k
                after = p_v[tile8(jnp.minimum(x + 1, XR - 1) if k == 7 else x + 1), :]
                then = east(x + 1, after, p)
                f = f_v[tile8(x + 1), :]
                north = f * pltpu.roll(f, 1, 1) * (n_v[tile8(x), :] - (p - pltpu.roll(p, 1, 1)))
                up = f * pltpu.roll(f, 1, 0) * (w_v[tile8(x), :] - (p - pltpu.roll(p, 1, 0)))
                up = jnp.where(sub == 0, 0.0, up)
                eo_v[tile8(x), :] = now
                no_v[tile8(x), :] = north
                wo_v[tile8(x), :] = up
                ro_v[tile8(x), :] = (now - then) + (north - pltpu.roll(north, NY - 1, 1)) + (up - pltpu.roll(up, 7, 0))
                now, p = then, after
            return 0

        lax.fori_loop(0, XR // 8, outputs, 0)

    with jax.named_scope("waitend"):
        for h in range(NH):
            wait_bytes(send1.at[pl.ds(h * NZ, NZ - 8)], a_s.at[h])
            wait_bytes(ag_v.at[pl.ds(h * XY * 2 * PR, (XY - 1) * 2 * PR)], g_s.at[h])
            wait_bytes(send2.at[pl.ds(h * NZ, NZ - 8)], b_s.at[h])
        halos[5].wait()
        for c in planes:
            c.wait()
    with jax.named_scope("faces"):
        west = f_v[pl.ds(8, 8), :] * fx_v[pl.ds(0, 8), :]
        west = west * (e_v[pl.ds(0, 8), :] - (p_v[pl.ds(0, 8), :] - px_v[pl.ds(0, 8), :]))
        east = f_v[pl.ds(ROWS, 8), :] * fx_v[pl.ds(8, 8), :]
        east = east * (ex_v[...] - (px_v[pl.ds(8, 8), :] - p_v[pl.ds(ROWS - 8, 8), :]))
        eo_v[pl.ds(0, 8), :] = west
        ro_v[pl.ds(0, 8), :] = ro_v[pl.ds(0, 8), :] + west
        ro_v[pl.ds(ROWS - 8, 8), :] = ro_v[pl.ds(ROWS - 8, 8), :] - east
        below = jnp.where(first, 0.0, zp_v[low, :])
        z0_v[...] = jnp.where(first, 1.0, zf_v[low, :]) * (gs_v[...] - zs_v[high, :] * (pb_v[low, :] - below))
        above = zs_v[low, :] * (ga_v[...] - zf_v[high, :] * (zp_v[high, :] - pb_v[high, :]))
        z7_v[...] = jnp.where(last, 0.0, above)


def last_kernel(p, e, n, w, r, z0, z7, eo, no, wo, po, ro, w_v, r_v, sem):
    copies = [pltpu.make_async_copy(src, dst, sem.at[k]) for k, (src, dst) in enumerate(((e, eo), (n, no), (p, po)))]
    for c in copies:
        c.start()
    sub = lax.broadcasted_iota(jnp.int32, (8, NY), 0)
    for s in range(XR // XS):

        def one(i, _):
            for k in range(8):
                x = s * XS + i * 8 + k
                face = row(z0, x)
                w_v[tile8(x), :] = jnp.where(sub == 0, face, w[tile8(x), :])
                r_v[tile8(x), :] = r[tile8(x), :] + jnp.where(sub == 0, face, jnp.where(sub == 7, -row(z7, x), 0.0))
            return 0

        lax.fori_loop(0, XS // 8, one, 0)
        rows = pl.ds(s * XS * 8, XS * 8)
        for k, (src, dst) in enumerate(((w_v, wo), (r_v, ro))):
            copy = pltpu.make_async_copy(src.at[rows], dst.at[rows], sem.at[3 + 2 * s + k])
            copy.start()
            copies.append(copy)
    for c in copies:
        c.wait()


def tables():
    i = np.arange(NY)
    angle = 2 * np.pi * ((i[:, None] * i[None, :]) % NY) / NY
    hart = np.cos(angle) + np.sin(angle)
    k = np.arange(1, NZ + 1)
    sine = np.sin(np.pi * ((k[:, None] * k[None, :]) % (2 * (NZ + 1))) / (NZ + 1))
    lam = 4 * np.sin(np.pi * i / NY) ** 2
    mu = 4 * np.sin(np.pi * k / (2 * (NZ + 1))) ** 2

    def cut(a):
        hi = a.astype(np.float32).astype(BF16)
        return hi, (a - hi.astype(np.float64)).astype(np.float32).astype(BF16)

    lanes_of = np.arange(128)
    half = np.arange(NH)[:, None, None]
    who = slot(np.arange(GZ))[None, :, None]
    lam = lam[half * LH + who * KL + lanes_of[None, None, :] % KL].reshape(NH * GZ, 128)
    packed = mu[(lanes_of[None, :] // KL) * PR + np.arange(PR)[:, None]]
    mu = np.repeat(mu[:, None], 128, 1)
    return (*cut(hart), *cut(sine), lam.astype(np.float32), mu.astype(np.float32), packed.astype(np.float32))


def local(east_velocity, north_velocity, upward_velocity, obstacle):
    fields = (east_velocity, north_velocity, upward_velocity, obstacle)
    args = [pltpu.with_memory_space_constraint(a.reshape(ROWS, NY), pltpu.HBM) for a in fields]
    args += [pltpu.with_memory_space_constraint(jnp.asarray(t), pltpu.HBM) for t in tables()]
    any_spec = pl.BlockSpec(memory_space=pl.ANY)
    vmem = pl.BlockSpec(memory_space=pltpu.VMEM)

    def v(*shape, dtype=F32):
        return pltpu.VMEM(shape, dtype)

    dma = pltpu.SemaphoreType.DMA
    field = jax.ShapeDtypeStruct((ROWS, NY), F32)
    plane = jax.ShapeDtypeStruct((XR, NY), F32)
    operands = pl.pallas_call(
        main_kernel,
        out_shape=[field] * 5 + [plane] * 2,
        in_specs=[any_spec] * 11,
        out_specs=[vmem] * 7,
        scratch_shapes=[
            v(ROWS + 16, NY), v(ROWS + 8, NY), v(ROWS, NY), v(ROWS, NY), v(2 * XR, NY), v(2 * XR, NY), v(XR, NY), v(16, NY),
            v(ROWS, NY, dtype=jnp.int32), v(ROWS, NY),
            v(NY, NY, dtype=BF16), v(NY, NY, dtype=BF16), v(NZ, NZ, dtype=BF16), v(NZ, NZ, dtype=BF16),
            v(NH * GZ, 128), v(NZ, 128), v(PR, 128),
            v(2 * XR, NY), v(XR, NY), v(16, NY), v(8, NY), v(EDGE, NY), v(NH, EDGE, LH), v(EDGE, LH), v(EDGE, NY),
            v(NH * NZ, 128), v(NH * NZ, 128),
            v(NH * ROWS, LH), v(NH * NZ, W), v(NH * NZ, W), v(NZ, W, dtype=BF16), v(NZ, W, dtype=BF16),
            v(NH * NZ, W), v(NH * NZ, 128), v(NH * NZ, 128), v(NH * NZ, 128), v(NH * NZ, 128),
            v(NH * XY * 2 * PR, 128), v(NH * NZ, W), v(NH * NZ, W), v(ROWS, LH),
            dma((11,)), dma((6,)), dma((6,)), dma((NH,)), dma((NH,)), dma((NH,)), dma((NH,)),
            dma((NH,)), dma((NH,)), dma((4,)), dma((4,)),
        ],
        compiler_params=pltpu.CompilerParams(
            collective_id=0, has_side_effects=True, vmem_limit_bytes=32 * 1024 * 1024
        ),
        name="main",
    )(*args)

    outs = pl.pallas_call(
        last_kernel,
        out_shape=[field] * 5,
        in_specs=[vmem] * 7,
        out_specs=[any_spec] * 5,
        scratch_shapes=[v(ROWS, NY), v(ROWS, NY), dma((3 + 2 * (XR // XS),))],
        compiler_params=pltpu.CompilerParams(vmem_limit_bytes=8 * 1024 * 1024),
        name="last",
    )(*operands)
    return tuple(a.reshape(XR, CZ, NY) for a in outs)


def solution(mesh):
    spec = P("xy", "gz", None)
    return jax.shard_map(local, mesh=mesh, in_specs=(spec,) * 4, out_specs=(spec,) * 5, check_vma=False)
```

time: 71.8 us -> 53.2 us (0.74)
  Pallas kernels: 71.1 us -> 52.5 us
    pallas_call x2, Pallas kernels: 71.1 us -> 52.5 us  [the longest x1 50.1 us: local(): pl.pallas_call(main_kernel, out_shape=[field] * 5 + [plane] * 2, in_specs...]
where the time goes in v3:
time: 53.2 us; the launch traced here: 53.1 us
  Pallas kernels  52.5 us (99%)
  between operations  0.64 us (1%)
    pallas_call x1, Pallas kernels, local(): pl.pallas_call(main_kernel, out_shape=[field] * 5 + [plane] * 2, in_specs...  50.1 us
    pallas_call x1, Pallas kernels, local(): pl.pallas_call(last_kernel, out_shape=[field] * 5, in_specs=[vmem] * 7, o...  2.42 us

profile of v3, /device:TPU:2, one launch (start us, length us, event | category | flops | bytes accessed | tf_op | source)
XLA Modules:
  0.0 53.1 jit_solution(5674514383652612575)
XLA Ops:
  0.6 50.1 %main.1 = (f32[512,512]{1,0:T(8,128)S(1)}, f32[512,512]{1,0:T(8,128)S(1)}, f32[512,512]{1,0:T(8,128)S(1)}, f32[512,512]{1,0:T(8,128)S(1)}, f32[512,512]{1,0:T(8,...) custom-call(f32[512,512]{1,0:T(8,128)} %bitcast.9, f32[512,512]{1,0:T(8,128)} %bitcast.10, f32[512,512]{1,0:T(8,128)} %bitcast.11, ...), custom_call_target="tpu_custom_call" | custom-call | tf_op jit(solution)/shard_map/main/pallas_call | solution.py:609
  50.7 2.4 %last.1 = (f32[512,512]{1,0:T(8,128)}, f32[512,512]{1,0:T(8,128)}, f32[512,512]{1,0:T(8,128)}, f32[512,512]{1,0:T(8,128)}, f32[512,512]{1,0:T(8,128)}) custom-call(f32[512,512]{1,0:T(8,128)S(1)} %get-tuple-element.17.p, f32[512,512]{1,0:T(8,128)S(1)} %get-tuple-element.18.e, f32[512,512]{1,0:T(8,128)S(1)} %get-tuple-element.19.n, ...), custom_call_target="tpu_custom_call" | custom-call | tf_op jit(solution)/shard_map/last/pallas_call | solution.py:633

commit v4 on v3

--- a/solution.py
+++ b/solution.py
@@ -93,9 +93,9 @@
 def main_kernel(
     e_h, n_h, w_h, o_h, hh_h, hl_h, sh_h, sl_h, lam_h, mu_h, mup_h,
     p_v, eo_v, no_v, wo_v, ro_v, z0_v, z7_v,
-    f_v, e_v, n_v, w_v, zp_v, zf_v, ga_v, px_v,
-    o_v, src_v, hh, hl, sh, sl, lam, mu, mup,
-    zs_v, gs_v, fx_v, ex_v, cc_v, cy_v, zb_v, pb_v, up_v, dn_v,
+    f_v, e_v, n_v, w_v, zf_v, ga_v,
+    o_v, src_h, src_l, hh, hl, sh, sl, lam, mu, mup,
+    zs_v, gs_v, fx_v, ex_v, cc_v, cc_h, cc_l, cy_v, zb_v, zq_v, ph_v, up_v, dn_v,
     y_v, send1, recv1, dh, dl, x_v, ea_v, eb_v, r_v, c_v, ag_v, send2, recv2, zz_v,
     load_sem, halo_s, halo_r, a_s, a_r, g_s, g_r, b_s, b_r, ph_s, ph_r,
 ):
@@ -129,10 +129,24 @@
         copy.start()
         return copy
 
+    class Shift:
+        def __init__(self, src, dst, ssem, rsem, up):
+            self.copy = pltpu.make_async_remote_copy(
+                src_ref=src, dst_ref=dst, send_sem=ssem, recv_sem=rsem, device_id=gz(1 if up else GZ - 1),
+                device_id_type=pl.DeviceIdType.MESH,
+            )
+            self.sends = me < GZ - 1 if up else me > 0
+            self.receives = me > 0 if up else me < GZ - 1
+            pl.when(self.sends)(lambda: self.copy.start())
+
+        def wait(self):
+            pl.when(self.receives)(lambda: self.copy.wait_recv())
+            pl.when(self.sends)(lambda: self.copy.wait_send())
+
     def wait_bytes(ref, sem):
         pltpu.make_async_copy(ref, ref, sem).wait()
 
-    flags = load(0, o_h, o_v)
+    flags, upward = load(0, o_h, o_v), load(1, w_h, w_v)
     barrier = pltpu.get_barrier_semaphore()
 
     def greet_gz(o, _):
@@ -143,12 +157,12 @@
         pl.semaphore_signal(barrier, inc=1, device_id=xy(o), device_id_type=pl.DeviceIdType.MESH)
         return 0
 
+    lax.fori_loop(1, XY, greet_xy, 0)
     lax.fori_loop(1, GZ, greet_gz, 0)
-    lax.fori_loop(1, XY, greet_xy, 0)
 
     loads = [
         flags,
-        load(1, w_h, w_v),
+        upward,
         load(2, e_h, e_v.at[pl.ds(0, ROWS)]),
         load(3, n_h, n_v),
         load(4, hh_h, hh),
@@ -184,17 +198,30 @@
             return 0
 
         lax.fori_loop(0, XR // 8, edge, 0)
-        loads[2].wait()
     with jax.named_scope("barrier"):
         pl.semaphore_wait(barrier, GZ - 1 + XY - 1)
     halos = [
-        remote(gs_v, ga_v, halo_s.at[0], halo_r.at[0], gz(GZ - 1)),
-        remote(zs_v.at[pl.ds(0, XR)], zf_v.at[pl.ds(0, XR)], halo_s.at[1], halo_r.at[1], gz(1)),
+        Shift(gs_v, ga_v, halo_s.at[0], halo_r.at[0], False),
+        Shift(zs_v.at[pl.ds(0, XR)], zf_v.at[pl.ds(0, XR)], halo_s.at[1], halo_r.at[1], True),
         remote(f_v.at[pl.ds(ROWS, 8)], fx_v.at[pl.ds(0, 8)], halo_s.at[2], halo_r.at[2], xy(1)),
         remote(f_v.at[pl.ds(8, 8)], fx_v.at[pl.ds(8, 8)], halo_s.at[3], halo_r.at[3], xy(XY - 1)),
-        remote(e_v.at[pl.ds(0, 8)], ex_v, halo_s.at[4], halo_r.at[4], xy(XY - 1)),
-        remote(zs_v.at[pl.ds(XR, XR)], zf_v.at[pl.ds(XR, XR)], halo_s.at[5], halo_r.at[5], gz(GZ - 1)),
+        Shift(zs_v.at[pl.ds(XR, XR)], zf_v.at[pl.ds(XR, XR)], halo_s.at[5], halo_r.at[5], False),
     ]
+    @pl.when(first)
+    def _():
+        zf_v[pl.ds(0, XR), :] = jnp.ones((XR, NY), F32)
+        for h in range(NH):
+            zq_v[pl.ds(h * EDGE, XR), :] = jnp.zeros((XR, LH), F32)
+
+    @pl.when(last)
+    def _():
+        ga_v[...] = jnp.zeros((XR, NY), F32)
+        zf_v[pl.ds(XR, XR), :] = jnp.zeros((XR, NY), F32)
+        for h in range(NH):
+            zq_v[pl.ds(h * EDGE + XR, XR), :] = jnp.zeros((XR, LH), F32)
+
+    loads[2].wait()
+    halos.append(remote(e_v.at[pl.ds(0, 8)], ex_v, halo_s.at[4], halo_r.at[4], xy(XY - 1)))
 
     with jax.named_scope("source"):
         loads[3].wait()
@@ -205,14 +232,19 @@
                 return f_v[tile8(x + 1), :] * f_v[tile8(x), :] * e_v[tile8(x), :]
 
             now = east(i * 8)
+            pair = []
             for k in range(8):
                 x = i * 8 + k
                 then = east(x + 1)
                 f = f_v[tile8(x + 1), :]
                 north = f * pltpu.roll(f, 1, 1) * n_v[tile8(x), :]
                 up = jnp.where(sub == 0, 0.0, f * pltpu.roll(f, 1, 0) * w_v[tile8(x), :])
-                src_v[tile8(x), :] = (now - then) + (north - pltpu.roll(north, NY - 1, 1)) + (up - pltpu.roll(up, 7, 0))
+                pair.append((now - then) + (north - pltpu.roll(north, NY - 1, 1)) + (up - pltpu.roll(up, 7, 0)))
                 now = then
+                if k % 2:
+                    rows = pl.ds(pl.multiple_of(i * 64 + (k - 1) * 8, 16), 16)
+                    src_h[rows, :], src_l[rows, :] = split(jnp.concatenate(pair, 0))
+                    pair = []
             return 0
 
         lax.fori_loop(0, XR // 8, source, 0)
@@ -222,35 +254,34 @@
             loads[k].wait()
 
         def forward(i, _):
-            y = dot3(split(src_v[pl.ds(pl.multiple_of(i * 128, 128), 128), :]), (hh[...], hl[...]))
+            rows = pl.ds(pl.multiple_of(i * 128, 128), 128)
+            y = dot3((src_h[rows, :], src_l[rows, :]), (hh[...], hl[...]))
             for h in range(NH):
-                out = pl.ds(pl.multiple_of(h * ROWS + i * 128, 128), 128)
-                y_v[out, :] = y[:, h * LH : h * LH + LH]
+                y_v[pl.ds(pl.multiple_of(h * ROWS + i * 128, 128), 128), :] = y[:, h * LH : h * LH + LH]
             return 0
 
         lax.fori_loop(0, ROWS // 128, forward, 0)
 
     with jax.named_scope("waithalo"):
-        for h in halos[:5]:
+        for h in (*halos[:4], halos[5]):
             h.wait()
 
     with jax.named_scope("edges"):
         low, high = pl.ds(0, XR), pl.ds(XR, XR)
-        cc_v[low, :] = jnp.where(first, 1.0, zf_v[low, :]) * gs_v[...]
-        cc_v[high, :] = jnp.where(last, 0.0, zs_v[low, :] * ga_v[...] * -1.0)
+        cc_v[low, :] = zf_v[low, :] * gs_v[...]
+        cc_v[high, :] = zs_v[low, :] * ga_v[...] * -1.0
         cc_v[pl.ds(2 * XR, 8), :] = fx_v[pl.ds(0, 8), :] * f_v[pl.ds(8, 8), :] * e_v[pl.ds(0, 8), :]
         cc_v[pl.ds(2 * XR + 8, 8), :] = f_v[pl.ds(ROWS, 8), :] * fx_v[pl.ds(8, 8), :] * ex_v[...] * -1.0
-        cy = dot3(split(cc_v[...]), (hh[...], hl[...]))
-        for h in range(NH):
-            part = cy[:, h * LH : h * LH + LH]
-            cy_v[h] = part
-            lo, hi = pl.ds(h * ROWS, 8), pl.ds(h * ROWS + ROWS - 8, 8)
-            y_v[lo, :] = y_v[lo, :] + part[2 * XR : 2 * XR + 8]
-            y_v[hi, :] = y_v[hi, :] + part[2 * XR + 8 :]
+        cc_h[...], cc_l[...] = split(cc_v[...])
 
     sub1 = lax.broadcasted_iota(jnp.int32, (8, 128), 0)
     for h in range(NH):
         with jax.named_scope("pack"):
+            hcol = pl.ds(h * LH, LH)
+            cy_v[...] = dot3((cc_h[...], cc_l[...]), (hh[:, hcol], hl[:, hcol]))
+            lo, hi = pl.ds(h * ROWS, 8), pl.ds(h * ROWS + ROWS - 8, 8)
+            y_v[lo, :] = y_v[lo, :] + cy_v[pl.ds(2 * XR, 8), :]
+            y_v[hi, :] = y_v[hi, :] + cy_v[pl.ds(2 * XR + 8, 8), :]
             mine = pl.ds(pl.multiple_of(h * NZ + me * 8, 8), 8)
             for t in range(NG):
                 tcol = pl.ds(t * 128, 128)
@@ -259,8 +290,8 @@
                     tiles = []
                     for a in range(XL):
                         x = a * J + j
-                        below = jnp.broadcast_to(cy_v[h, pl.ds(x, 1), tcol], (8, 128))
-                        above = jnp.broadcast_to(cy_v[h, pl.ds(XR + x, 1), tcol], (8, 128))
+                        below = jnp.broadcast_to(cy_v[pl.ds(x, 1), tcol], (8, 128))
+                        above = jnp.broadcast_to(cy_v[pl.ds(XR + x, 1), tcol], (8, 128))
                         extra = jnp.where(sub1 == 0, below, jnp.where(sub1 == 7, above, 0.0))
                         tiles.append(y_v[pl.ds((h * XR + x) * 8, 8), tcol] + extra)
                     tiles = exchange_lanes(tiles)
@@ -454,6 +485,17 @@
         if k >= LAG:
             ascend(k - LAG)
 
+    def neighbours():
+        total = None
+        for h in range(NH):
+            for c in planes[h]:
+                c.wait()
+            rows, hrow = pl.ds(h * EDGE, EDGE), pl.ds(h * LH, LH)
+            part = dot3(split(zb_v[rows, :] - zq_v[rows, :]), (hh[hrow, :], hl[hrow, :]))
+            total = part if h == 0 else total + part
+        ph_v[...] = total
+
+    planes = []
     for h in range(NH):
         hrow = pl.ds(h * LH, LH)
         with jax.named_scope("waitback"):
@@ -469,26 +511,31 @@
                         zz_v[pl.ds((a * J + j) * 8, 8), pl.ds(t * 128, 128)] = tiles[a]
 
         with jax.named_scope("planes"):
+            edge0 = h * EDGE
+
             def border(i, _):
                 for k in range(8):
                     x = i * 8 + k
-                    zb_v[pl.ds(x, 1), :] = zz_v[pl.ds(x * 8, 1), :]
-                    zb_v[pl.ds(XR + x, 1), :] = zz_v[pl.ds(x * 8 + 7, 1), :]
+                    zb_v[pl.ds(edge0 + x, 1), :] = zz_v[pl.ds(x * 8, 1), :]
+                    zb_v[pl.ds(edge0 + XR + x, 1), :] = zz_v[pl.ds(x * 8 + 7, 1), :]
                 return 0
 
             lax.fori_loop(0, XR // 8, border, 0)
-            zb_v[pl.ds(2 * XR, 8), :] = zz_v[pl.ds(0, 8), :]
-            zb_v[pl.ds(2 * XR + 8, 8), :] = zz_v[pl.ds(ROWS - 8, 8), :]
-            part = dot3(split(zb_v[...]), (hh[hrow, :], hl[hrow, :]))
-            pb_v[...] = part if h == 0 else pb_v[...] + part
-
-        if h == NH - 1:
-            planes = [
-                remote(pb_v.at[pl.ds(XR, XR)], zp_v.at[pl.ds(0, XR)], ph_s.at[0], ph_r.at[0], gz(1)),
-                remote(pb_v.at[pl.ds(0, XR)], zp_v.at[pl.ds(XR, XR)], ph_s.at[1], ph_r.at[1], gz(GZ - 1)),
-                remote(pb_v.at[pl.ds(2 * XR + 8, 8)], px_v.at[pl.ds(0, 8)], ph_s.at[2], ph_r.at[2], xy(1)),
-                remote(pb_v.at[pl.ds(2 * XR, 8)], px_v.at[pl.ds(8, 8)], ph_s.at[3], ph_r.at[3], xy(XY - 1)),
-            ]
+            zb_v[pl.ds(edge0 + 2 * XR, 8), :] = zz_v[pl.ds(0, 8), :]
+            zb_v[pl.ds(edge0 + 2 * XR + 8, 8), :] = zz_v[pl.ds(ROWS - 8, 8), :]
+            routes = (
+                (XR, 0, XR, True),
+                (0, XR, XR, False),
+                (2 * XR + 8, 2 * XR, 8, xy(1)),
+                (2 * XR, 2 * XR + 8, 8, xy(XY - 1)),
+            )
+            planes.append([
+                (Shift if k < 2 else remote)(
+                    zb_v.at[pl.ds(edge0 + a, size)], zq_v.at[pl.ds(edge0 + b, size)],
+                    ph_s.at[4 * h + k], ph_r.at[4 * h + k], who,
+                )
+                for k, (a, b, size, who) in enumerate(routes)
+            ])
 
         with jax.named_scope("inverse"):
             def inverse(i, _):
@@ -501,6 +548,7 @@
             lax.fori_loop(0, ROWS // 256, inverse, 0)
 
     with jax.named_scope("outputs"):
+
         def outputs(i, _):
             def east(x, p, before):
                 return f_v[tile8(x + 1), :] * f_v[tile8(x), :] * (e_v[tile8(x), :] - (p - before))
@@ -529,27 +577,31 @@
             wait_bytes(send1.at[pl.ds(h * NZ, NZ - 8)], a_s.at[h])
             wait_bytes(ag_v.at[pl.ds(h * XY * 2 * PR, (XY - 1) * 2 * PR)], g_s.at[h])
             wait_bytes(send2.at[pl.ds(h * NZ, NZ - 8)], b_s.at[h])
-        halos[5].wait()
-        for c in planes:
-            c.wait()
+        halos[4].wait()
+        neighbours()
     with jax.named_scope("faces"):
         west = f_v[pl.ds(8, 8), :] * fx_v[pl.ds(0, 8), :]
-        west = west * (e_v[pl.ds(0, 8), :] - (p_v[pl.ds(0, 8), :] - px_v[pl.ds(0, 8), :]))
+        west = west * (e_v[pl.ds(0, 8), :] - ph_v[pl.ds(2 * XR, 8), :])
         east = f_v[pl.ds(ROWS, 8), :] * fx_v[pl.ds(8, 8), :]
-        east = east * (ex_v[...] - (px_v[pl.ds(8, 8), :] - p_v[pl.ds(ROWS - 8, 8), :]))
+        east = east * (ex_v[...] + ph_v[pl.ds(2 * XR + 8, 8), :])
         eo_v[pl.ds(0, 8), :] = west
         ro_v[pl.ds(0, 8), :] = ro_v[pl.ds(0, 8), :] + west
         ro_v[pl.ds(ROWS - 8, 8), :] = ro_v[pl.ds(ROWS - 8, 8), :] - east
-        below = jnp.where(first, 0.0, zp_v[low, :])
-        z0_v[...] = jnp.where(first, 1.0, zf_v[low, :]) * (gs_v[...] - zs_v[high, :] * (pb_v[low, :] - below))
-        above = zs_v[low, :] * (ga_v[...] - zf_v[high, :] * (zp_v[high, :] - pb_v[high, :]))
-        z7_v[...] = jnp.where(last, 0.0, above)
+        z0_v[...] = zf_v[low, :] * (gs_v[...] - zs_v[high, :] * ph_v[low, :])
+        z7_v[...] = zs_v[low, :] * (ga_v[...] + zf_v[high, :] * ph_v[high, :])
 
 
 def last_kernel(p, e, n, w, r, z0, z7, eo, no, wo, po, ro, w_v, r_v, sem):
-    copies = [pltpu.make_async_copy(src, dst, sem.at[k]) for k, (src, dst) in enumerate(((e, eo), (n, no), (p, po)))]
-    for c in copies:
-        c.start()
+    copies = []
+
+    def out(src, dst, part):
+        rows = pl.ds(part * XS * 8, XS * 8)
+        copies.append(pltpu.make_async_copy(src.at[rows], dst.at[rows], sem.at[len(copies)]))
+        copies[-1].start()
+
+    for src, dst in ((e, eo), (n, no), (p, po)):
+        for part in range(XR // XS):
+            out(src, dst, part)
     sub = lax.broadcasted_iota(jnp.int32, (8, NY), 0)
     for s in range(XR // XS):
 
@@ -562,11 +614,8 @@
             return 0
 
         lax.fori_loop(0, XS // 8, one, 0)
-        rows = pl.ds(s * XS * 8, XS * 8)
-        for k, (src, dst) in enumerate(((w_v, wo), (r_v, ro))):
-            copy = pltpu.make_async_copy(src.at[rows], dst.at[rows], sem.at[3 + 2 * s + k])
-            copy.start()
-            copies.append(copy)
+        out(w_v, wo, s)
+        out(r_v, ro, s)
     for c in copies:
         c.wait()
 
@@ -612,17 +661,17 @@
         in_specs=[any_spec] * 11,
         out_specs=[vmem] * 7,
         scratch_shapes=[
-            v(ROWS + 16, NY), v(ROWS + 8, NY), v(ROWS, NY), v(ROWS, NY), v(2 * XR, NY), v(2 * XR, NY), v(XR, NY), v(16, NY),
-            v(ROWS, NY, dtype=jnp.int32), v(ROWS, NY),
+            v(ROWS + 16, NY), v(ROWS + 8, NY), v(ROWS, NY), v(ROWS, NY), v(2 * XR, NY), v(XR, NY),
+            v(ROWS, NY, dtype=jnp.int32), v(ROWS, NY, dtype=BF16), v(ROWS, NY, dtype=BF16),
             v(NY, NY, dtype=BF16), v(NY, NY, dtype=BF16), v(NZ, NZ, dtype=BF16), v(NZ, NZ, dtype=BF16),
             v(NH * GZ, 128), v(NZ, 128), v(PR, 128),
-            v(2 * XR, NY), v(XR, NY), v(16, NY), v(8, NY), v(EDGE, NY), v(NH, EDGE, LH), v(EDGE, LH), v(EDGE, NY),
+            v(2 * XR, NY), v(XR, NY), v(16, NY), v(8, NY), v(EDGE, NY), v(EDGE, NY, dtype=BF16), v(EDGE, NY, dtype=BF16), v(EDGE, LH), v(NH * EDGE, LH), v(NH * EDGE, LH), v(EDGE, NY),
             v(NH * NZ, 128), v(NH * NZ, 128),
             v(NH * ROWS, LH), v(NH * NZ, W), v(NH * NZ, W), v(NZ, W, dtype=BF16), v(NZ, W, dtype=BF16),
             v(NH * NZ, W), v(NH * NZ, 128), v(NH * NZ, 128), v(NH * NZ, 128), v(NH * NZ, 128),
             v(NH * XY * 2 * PR, 128), v(NH * NZ, W), v(NH * NZ, W), v(ROWS, LH),
             dma((11,)), dma((6,)), dma((6,)), dma((NH,)), dma((NH,)), dma((NH,)), dma((NH,)),
-            dma((NH,)), dma((NH,)), dma((4,)), dma((4,)),
+            dma((NH,)), dma((NH,)), dma((4 * NH,)), dma((4 * NH,)),
         ],
         compiler_params=pltpu.CompilerParams(
             collective_id=0, has_side_effects=True, vmem_limit_bytes=32 * 1024 * 1024
@@ -635,7 +684,7 @@
         out_shape=[field] * 5,
         in_specs=[vmem] * 7,
         out_specs=[any_spec] * 5,
-        scratch_shapes=[v(ROWS, NY), v(ROWS, NY), dma((3 + 2 * (XR // XS),))],
+        scratch_shapes=[v(ROWS, NY), v(ROWS, NY), dma((5 * (XR // XS),))],
         compiler_params=pltpu.CompilerParams(vmem_limit_bytes=8 * 1024 * 1024),
         name="last",
     )(*operands)

time: 53.2 us -> 52.1 us (0.979)
  Pallas kernels: 52.5 us -> 51 us
    pallas_call x1, Pallas kernels: 50.1 us -> 48.5 us  [local(): pl.pallas_call(main_kernel, out_shape=[field] * 5 + [plane] * 2, in_specs...]
where the time goes in v4:
time: 52.1 us; the launch traced here: 51.6 us
  Pallas kernels  51 us (98%)
  between operations  0.64 us (1%)
    pallas_call x1, Pallas kernels, local(): pl.pallas_call(main_kernel, out_shape=[field] * 5 + [plane] * 2, in_specs...  48.5 us
    pallas_call x1, Pallas kernels, local(): pl.pallas_call(last_kernel, out_shape=[field] * 5, in_specs=[vmem] * 7, o...  2.49 us

profile of v4, /device:TPU:2, one launch (start us, length us, event | category | flops | bytes accessed | tf_op | source)
XLA Modules:
  0.0 51.6 jit_solution(16746924314278686846)
XLA Ops:
  0.6 48.5 %main.1 = (f32[512,512]{1,0:T(8,128)S(1)}, f32[512,512]{1,0:T(8,128)S(1)}, f32[512,512]{1,0:T(8,128)S(1)}, f32[512,512]{1,0:T(8,128)S(1)}, f32[512,512]{1,0:T(8,...) custom-call(f32[512,512]{1,0:T(8,128)} %bitcast.9, f32[512,512]{1,0:T(8,128)} %bitcast.10, f32[512,512]{1,0:T(8,128)} %bitcast.11, ...), custom_call_target="tpu_custom_call" | custom-call | tf_op jit(solution)/shard_map/main/pallas_call | solution.py:658
  49.1 2.5 %last.1 = (f32[512,512]{1,0:T(8,128)}, f32[512,512]{1,0:T(8,128)}, f32[512,512]{1,0:T(8,128)}, f32[512,512]{1,0:T(8,128)}, f32[512,512]{1,0:T(8,128)}) custom-call(f32[512,512]{1,0:T(8,128)S(1)} %get-tuple-element.17.p, f32[512,512]{1,0:T(8,128)S(1)} %get-tuple-element.18.e, f32[512,512]{1,0:T(8,128)S(1)} %get-tuple-element.19.n, ...), custom_call_target="tpu_custom_call" | custom-call | tf_op jit(solution)/shard_map/last/pallas_call | solution.py:682

commit v5 on v4

--- a/solution.py
+++ b/solution.py
@@ -24,7 +24,7 @@
 ROWS = XR * CZ
 LOGJ = J.bit_length() - 1
 BR = 32
-BW = 128
+BW = 256
 NG = LH // 128
 PR = NZ // XL
 LAG = 2
@@ -404,11 +404,8 @@
             ag_v[pl.ds(at, PR), :] = pa
             ag_v[pl.ds(pl.multiple_of(at + PR, PR), PR), :] = pb
 
-            def spread(o, _):
+            for o in sorted(range(1, XY), key=lambda o: -min(o, XY - o)):
                 remote(ag_v.at[own], ag_v.at[own], g_s.at[h], g_r.at[h], xy(o))
-                return 0
-
-            lax.fori_loop(1, XY, spread, 0)
 
     def ascend(h):
         with jax.named_scope("waitgather"):

time: 52.1 us -> 51.8 us (level)
  no operation moved by 1% of the time
where the time goes in v5:
time: 51.8 us; the launch traced here: 51.2 us
  Pallas kernels  50.6 us (98%)
  between operations  0.64 us (1%)
    pallas_call x1, Pallas kernels, local(): pl.pallas_call(main_kernel, out_shape=[field] * 5 + [plane] * 2, in_specs...  48.1 us
    pallas_call x1, Pallas kernels, local(): pl.pallas_call(last_kernel, out_shape=[field] * 5, in_specs=[vmem] * 7, o...  2.49 us

profile of v5, /device:TPU:2, one launch (start us, length us, event | category | flops | bytes accessed | tf_op | source)
XLA Modules:
  0.0 51.2 jit_solution(14047649770473557357)
XLA Ops:
  0.6 48.1 %main.1 = (f32[512,512]{1,0:T(8,128)S(1)}, f32[512,512]{1,0:T(8,128)S(1)}, f32[512,512]{1,0:T(8,128)S(1)}, f32[512,512]{1,0:T(8,128)S(1)}, f32[512,512]{1,0:T(8,...) custom-call(f32[512,512]{1,0:T(8,128)} %bitcast.9, f32[512,512]{1,0:T(8,128)} %bitcast.10, f32[512,512]{1,0:T(8,128)} %bitcast.11, ...), custom_call_target="tpu_custom_call" | custom-call | tf_op jit(solution)/shard_map/main/pallas_call | solution.py:655
  48.7 2.5 %last.1 = (f32[512,512]{1,0:T(8,128)}, f32[512,512]{1,0:T(8,128)}, f32[512,512]{1,0:T(8,128)}, f32[512,512]{1,0:T(8,128)}, f32[512,512]{1,0:T(8,128)}) custom-call(f32[512,512]{1,0:T(8,128)S(1)} %get-tuple-element.17.p, f32[512,512]{1,0:T(8,128)S(1)} %get-tuple-element.18.e, f32[512,512]{1,0:T(8,128)S(1)} %get-tuple-element.19.n, ...), custom_call_target="tpu_custom_call" | custom-call | tf_op jit(solution)/shard_map/last/pallas_call | solution.py:679
